TPU v7x, 128 devices: a whole 4x4x4 slice. The times are simulated.
128 devices in a mesh: dp: 32 (over z, y, core), mp: 4 (over x).
Axes of the slice: x: 4, y: 4, z: 4, core: 2. Of those that a mesh axis runs over, the one named last changes fastest.
Arguments:
- queries: bfloat16 [1024, 64, 128], P('dp', 'mp'), may hold values from -8 to 8
- lookup_sheets: bfloat16 [32768, 16, 8, 128], P('dp', None, 'mp'), may hold values from -6 to 6
- content_sheets: bfloat16 [32768, 16, 8, 128], P('dp', None, 'mp'), may hold values from -12 to 12
- page_table: int32 [1024, 32], replicated, may hold values from 0 to 32767, as said below
- context_len: int32 [1024], replicated, may hold values from 32 to 512, as said below
- out_weight: bfloat16 [8192, 8192], P('mp', 'dp'), may hold values from -0.0625 to 0.0625
Outputs:
- attention: bfloat16 [1024, 64, 128], P('dp', 'mp')
- projected: bfloat16 [1024, 8192], P('mp', 'dp')
Inputs may be any that keep to these rules, and one draw needn't show every extreme that they name: `page_table`: every entry names a pool page, 0 to 32767, and every pool page appears exactly once in the whole table. `context_len`: each length lies between 32 and 512; most contexts are short, and some request has exactly 512 tokens.
All inputs are finite; a program needn't handle non-finite values.
Results may differ from a plain program's by a relative error of at most 0.0015.
Values may be sent and summed in bfloat16 or wider, within the bound.
A program may use at most 128 MiB of HBM per device.

v0:
```python
import functools

import jax
import jax.numpy as jnp
from jax import lax
from jax.sharding import Mesh
from jax.sharding import PartitionSpec as P

DP = ("dp_0", "dp_1", "dp_2")


def for_sending(array):
    return jax.tree.map(lambda a: a.astype(jnp.bfloat16) if a.dtype == jnp.float32 else a, array)


def one_axis_at_a_time(array, axes):
    return functools.reduce(lax.pmax, axes, array)


def pick_rows(onehot_f, table):
    flat = table.reshape(table.shape[0], -1)
    picked = jnp.dot(
        onehot_f, flat, preferred_element_type=jnp.float32, precision=lax.Precision.HIGHEST
    )
    return picked.reshape((onehot_f.shape[0],) + table.shape[1:])


def sum_rows(onehot_t, table):
    flat = table.reshape(table.shape[0], -1)
    summed = jnp.dot(
        onehot_t, flat, preferred_element_type=jnp.float32, precision=lax.Precision.HIGHEST
    )
    return summed.reshape((onehot_t.shape[0],) + table.shape[1:])


def body(queries, lookup_sheets, content_sheets, page_table, context_len, out_weight):
    req_rows = page_table.shape[0]
    max_pages = page_table.shape[1]
    pool_local, page_len, kv_local, head_dim = lookup_sheets.shape
    q_local = queries.shape[1]
    cluster_member = q_local // kv_local
    dp_count = lax.axis_size(DP)
    rows_mine = req_rows // dp_count
    first_page = lax.axis_index(DP) * pool_local
    local_ids = first_page + jnp.arange(pool_local, dtype=jnp.int32)
    table_blocks = page_table.reshape(dp_count, rows_mine, max_pages)
    block_starts = jnp.arange(dp_count, dtype=jnp.int32) * rows_mine
    row_numbers = jnp.arange(rows_mine, dtype=jnp.int32)
    column_numbers = jnp.arange(max_pages, dtype=jnp.int32)

    def find_owner(carry, inputs):
        table_block, block_start = inputs
        matched = (table_block[None, :, :] == local_ids[:, None, None]).astype(jnp.int32)
        owner_add = jnp.sum(matched * (block_start + row_numbers)[None, :, None], axis=(1, 2))
        slot_add = jnp.sum(matched * column_numbers[None, None, :], axis=(1, 2))
        return ((carry[0] + owner_add, carry[1] + slot_add), None)

    zeros_local = jnp.zeros((pool_local,), jnp.int32)
    (owners, page_slot), unused = lax.scan(
        find_owner, (zeros_local, zeros_local), (table_blocks, block_starts)
    )
    onehot = owners[:, None] == jnp.arange(req_rows, dtype=jnp.int32)[None, :]
    onehot_f = onehot.astype(jnp.float32)
    onehot_t = jnp.transpose(onehot_f)
    all_queries = lax.all_gather(queries, DP, axis=0, tiled=True)
    page_queries = jnp.dot(
        onehot.astype(jnp.bfloat16),
        all_queries.reshape(req_rows, q_local * head_dim),
        preferred_element_type=jnp.float32,
    ).astype(jnp.bfloat16)
    page_queries = page_queries.reshape(pool_local, kv_local, cluster_member, head_dim)
    scores = jnp.einsum(
        "pkgd,ptkd->pkgt", page_queries, lookup_sheets, preferred_element_type=jnp.float32
    ) * head_dim ** (-0.5)
    page_length = jnp.sum(jnp.where(onehot, context_len[None, :], 0), axis=1)
    position = page_slot[:, None] * page_len + jnp.arange(page_len, dtype=jnp.int32)[None, :]
    is_valid = (position < page_length[:, None])[:, None, None, :]
    scores = jnp.where(is_valid, scores, -1e30)
    page_peak = jnp.max(scores, axis=3)
    weights = jnp.where(is_valid, jnp.exp(scores - page_peak[..., None]), 0.0)
    page_mass = jnp.sum(weights, axis=3)
    page_acc = jnp.einsum(
        "pkgt,ptkd->pkgd",
        weights.astype(jnp.bfloat16),
        content_sheets,
        preferred_element_type=jnp.float32,
    )
    local_peak = jnp.max(
        jnp.where(onehot[:, :, None, None], page_peak[:, None, :, :], -1e30), axis=0
    )
    peak_all = one_axis_at_a_time(for_sending(local_peak), DP).astype(local_peak.dtype)
    factor = jnp.exp(page_peak - pick_rows(onehot_f, peak_all))
    mass_sum = sum_rows(onehot_t, page_mass * factor)
    acc_sum = sum_rows(onehot_t, page_acc * factor[..., None])
    acc_mine, mass_mine = (
        lax.psum_scatter(acc_sum, DP, scatter_dimension=0, tiled=True),
        lax.psum_scatter(mass_sum, DP, scatter_dimension=0, tiled=True),
    )
    attention = (
        (acc_mine / mass_mine[..., None]).astype(jnp.bfloat16).reshape(rows_mine, q_local, head_dim)
    )
    flat_attention = attention.reshape(rows_mine, q_local * head_dim)

    def project(block_rows):
        return jnp.dot(block_rows, out_weight, preferred_element_type=jnp.float32)

    partial_value = project(lax.all_gather(flat_attention, DP, axis=0, tiled=True))
    projected = lax.psum_scatter(partial_value, "mp", scatter_dimension=0, tiled=True).astype(
        jnp.bfloat16
    )
    return (attention, projected)


def solution(mesh):
    finer = Mesh(mesh.devices.reshape(4, 4, 2, mesh.shape["mp"]), ("dp_0", "dp_1", "dp_2", "mp"))
    return jax.shard_map(
        body,
        mesh=finer,
        in_specs=(
            P(DP, "mp", None),
            P(DP, None, "mp", None),
            P(DP, None, "mp", None),
            P(),
            P(),
            P("mp", DP),
        ),
        out_specs=(P(DP, "mp", None), P("mp", DP)),
        check_vma=False,
    )
```

profile of v0, /device:TPU:1, one launch (start us, length us, event | category | flops | bytes accessed | tf_op | source)
XLA Modules:
  0.0 437.8 jit_solution(16308813133409433919)
XLA Ops:
  7.2 0.7 all-gather.3.cloned.1.call-update
  8.0 1.1 copy.37
  9.1 68.5 %while.15 = (s32[]{:T(128)}, s32[1024]{0:T(1024)S(1)}, s32[1024]{0:T(1024)S(1)}, s32[32,32,32]{2,1,0:T(8,128)S(1)}, s32[32]{0:T(128)S(1)}, /*index=5*/s32[]{:T(128)}, s32[]{:T(128)}, s32[]{:T(128)}) while((s32[]{:T(128)}, s32[1024]{0:T(1024)S(1)}, s32[1024]{0:T(1024)S(1)}, s32[32,32,32]{2,1,0:T(8,128)S(1)}, ...), condition=%wide.region_3.4_spmd.clone.clone, body=%wide.region_0.3_spmd.clone.clone.sunk | while | flops 5245987 | bytes 53623 | solution.py:59
  9.7 0.6 iota_add_fusion.5
  10.4 0.8 fusion.62
  12.5 0.8 fusion.62
  14.7 0.8 fusion.62
  16.8 0.8 fusion.62
  18.9 0.8 fusion.62
  21.1 0.8 fusion.62
  23.2 0.8 fusion.62
  25.4 0.8 fusion.62
  27.5 0.8 fusion.62
  29.6 0.8 fusion.62
  31.8 0.8 fusion.62
  33.9 0.8 fusion.62
  36.1 0.8 fusion.62
  38.2 0.8 fusion.62
  40.3 0.8 fusion.62
  42.5 0.8 fusion.62
  44.6 0.8 fusion.62
  46.8 0.8 fusion.62
  48.9 0.8 fusion.62
  51.0 0.8 fusion.62
  53.2 0.8 fusion.62
  55.3 0.8 fusion.62
  57.5 0.8 fusion.62
  59.6 0.8 fusion.62
  61.7 0.8 fusion.62
  63.9 0.8 fusion.62
  66.0 0.8 fusion.62
  68.2 0.8 fusion.62
  70.3 0.8 fusion.62
  72.4 0.8 fusion.62
  74.6 0.8 fusion.62
  76.7 0.8 fusion.62
  77.6 1.4 select_reduce_fusion.1
  79.4 0.7 iota_compare_fusion
  80.1 7.2 %convert_bitcast_fusion = bf16[128,8,16,128]{3,1,2,0:T(8,128)(2,1)S(1)} fusion(bf16[128,8,16,128]{3,2,1,0:T(8,128)(2,1)} %bitcast.79, s32[1024]{0:T(1024)S(1)} %get-tuple-element.63), kind=kOutput, calls=%fused_computation.30 | convolution fusion | flops 4298113024 | bytes 8392704 | tf_op jit(solution)/shard_map/dot_general | solution.py:66
  87.3 1.4 copy.54
  88.7 9.5 %fusion.10 = (f32[1024,2,8]{2,1,0:T(2,128)S(1)}, f32[1024,2,8,16]{3,2,1,0:T(8,128)}) fusion(pred[1024,16]{1,0:T(8,128)(4,1)S(1)} %add_compare_fusion, bf16[1024,2,8,128]{3,2,1,0:T(8,128)(2,1)S(1)} %bitcast.70, bf16[1024,16,2,128]{3,2,1,0:T(2,128)(2,1)} %param.9), kind=kOutput, calls=%fused_computation.19 | convolution fusion | flops 67878912 | bytes 13713408 | tf_op jit(solution)/shard_map/pkgd,ptkd->pkgt/dot_general | solution.py:72
  98.6 31.2 %fusion.11 = f32[1024,2,8]{2,1,0:T(2,128)} fusion(f32[1024,2,8,16]{3,2,1,0:T(8,128)} %get-tuple-element.134, f32[1024,2,8]{2,1,0:T(2,128)S(1)} %get-tuple-element.133, pred[1024,16]{1,0:T(8,128)(4,1)S(1)} %add_compare_fusion), kind=kLoop, calls=%fused_computation.20 | loop fusion | flops 1294336 | bytes 1196032 | tf_op jit(solution)/shard_map/reduce_sum | solution.py:81
  129.8 1.4 copy.44
  131.1 9.0 %select_reduce_fusion = bf16[1024,2,8]{0,2,1:T(8,128)(2,1)S(1)} fusion(f32[1024,2,8]{2,1,0:T(2,128)S(1)} %get-tuple-element.133, pred[1024,1024]{1,0:T(8,128)(4,1)S(1)} %iota_compare_fusion), kind=kLoop, calls=%fused_computation.11 | loop fusion | flops 33538048 | bytes 1146880 | tf_op jit(solution)/shard_map/reduce_max | solution.py:88
  140.1 15.4 %pmax.21 = bf16[1024,2,8]{0,2,1:T(8,128)(2,1)S(1)} all-reduce(bf16[1024,2,8]{0,2,1:T(8,128)(2,1)S(1)} %select_reduce_fusion), channel_id=1, replica_groups=mesh['dp_0'=4,'dp_1'=4,'dp_2'=2,'mp'=4] {'dp_0'}, use_global_device_ids=true, to_apply=%region_7.8 | all-reduce | flops 16384 | bytes 65536 | tf_op jit(solution)/shard_map/pmax | solution.py:17
  155.5 13.6 %pmax.22 = bf16[1024,2,8]{0,2,1:T(8,128)(2,1)S(1)} all-reduce(bf16[1024,2,8]{0,2,1:T(8,128)(2,1)S(1)} %pmax.21), channel_id=1, replica_groups=mesh['dp_0'=4,'dp_1'=4,'dp_2'=2,'mp'=4] {'dp_1'}, use_global_device_ids=true, to_apply=%region_8.9 | all-reduce | flops 16384 | bytes 65536 | tf_op jit(solution)/shard_map/pmax | solution.py:17
  169.1 11.4 %pmax.23 = bf16[2,8,1024]{2,1,0:T(8,128)(2,1)S(1)} all-reduce(bf16[2,8,1024]{2,1,0:T(8,128)(2,1)S(1)} %bitcast.77), channel_id=1, replica_groups=mesh['dp_0'=4,'dp_1'=4,'dp_2'=2,'mp'=4] {'dp_2'}, use_global_device_ids=true, to_apply=%region_9.10 | all-reduce | flops 16384 | bytes 65536 | tf_op jit(solution)/shard_map/pmax | solution.py:17
  180.6 0.9 fusion.44
  182.0 1.5 fusion.47
  183.5 1.0 copy.51
  184.6 12.5 %broadcast_multiply_fusion = f32[1024,2,8,128]{3,2,1,0:T(8,128)S(1)} fusion(f32[1024,2,8]{2,1,0:T(2,128)S(1)} %copy.41, bf16[1024,16,2,128]{3,2,1,0:T(2,128)(2,1)} %param.10, f32[1024,2,8,16]{3,2,1,0:T(8,128)} %get-tuple-element.134, f32[1024,2,8]{2,1,0:T(2,128)S(1)} %get-tuple-element.133, pred[1024,16]{1,0:T(8,128)(4,1)S(1)} %add_compare_fusion), kind=kOutput, calls=%fused_computation.25 | convolution fusion | flops 70516736 | bytes 17973248 | tf_op jit(solution)/shard_map/pkgt,ptkd->pkgd/dot_general | solution.py:82
  197.0 7.3 %copy.73 = f32[128,8,16,128]{3,1,2,0:T(8,128)} copy(f32[128,8,16,128]{3,2,1,0:T(8,128)S(1)} %bitcast.71) | data formatting | bytes 16777216
  204.4 9.3 %copy.42 = f32[2048,1024]{1,0:T(8,128)} copy(f32[2048,1024]{0,1:T(8,128)} %bitcast.69) | data formatting | bytes 16777216 | tf_op jit(solution)/shard_map/dot_general | solution.py:30
  213.6 20.1 %fusion.35 = f32[1024,2,8,128]{3,0,2,1:T(8,128)} fusion(f32[2,8,128,1024]{3,2,1,0:T(8,128)} %bitcast.72, s32[1024]{0:T(1024)S(1)} %get-tuple-element.63), kind=kOutput, calls=%fused_computation.39 | convolution fusion | flops 25771900928 | bytes 16781312 | tf_op jit(solution)/shard_map/dot_general | solution.py:30
  233.8 24.1 %reduce-scatter.10.cloned.1.call-done = f32[32,16]{1,0:T(8,128)} async-done(((f32[1024,16]{1,0:T(8,128)}), f32[32,16]{1,0:T(8,128)}) %reduce-scatter.10.cloned.1.call-update) | async-done | bytes 2064
  257.9 0.8 copy.52
  258.7 95.3 %reduce-scatter.6.cloned.1.call-done = f32[32,2,8,128]{3,0,2,1:T(8,128)} async-done(((f32[1024,2,8,128]{3,0,2,1:T(8,128)}), f32[32,2,8,128]{3,0,2,1:T(8,128)}) %reduce-scatter.6.cloned.1.call-update) | async-done | bytes 262160 | tf_op jit(solution)/shard_map/reduce_scatter | solution.py:96
  354.0 1.1 divide_convert_fusion
  355.2 0.7 copy.74
  355.9 48.4 %all-gather.5.cloned.1.call-done = bf16[1024,2048]{1,0:T(8,128)(2,1)} async-done(((bf16[32,2048]{1,0:T(8,128)(2,1)}), bf16[1024,2048]{1,0:T(8,128)(2,1)}) %all-gather.5.cloned.1.call-update) | async-done | bytes 4194320 | tf_op jit(solution)/shard_map/all_gather | solution.py:107
  404.3 4.4 %fusion.55 = f32[1024,256]{1,0:T(8,128)} fusion(bf16[1024,2048]{1,0:T(8,128)(2,1)} %all-gather.5.cloned.1.call-done, bf16[2048,256]{1,0:T(8,128)(2,1)S(1)} %copy-done), kind=kOutput, calls=%fused_computation.57 | convolution fusion | flops 1073741824 | bytes 6291456 | tf_op jit(solution)/shard_map/dot_general | solution.py:105
  408.8 0.7 copy.46
  409.5 20.2 %reduce-scatter.8.cloned.1.call-done = f32[256,256]{1,0:T(8,128)} async-done(((f32[1024,256]{1,0:T(8,128)}), f32[256,256]{1,0:T(8,128)}) %reduce-scatter.8.cloned.1.call-update) | async-done | bytes 262160 | tf_op jit(solution)/shard_map/reduce_scatter | solution.py:108
  429.7 1.6 convert_element_type.24
  (179 shorter events, 40.6 us)
Async XLA Ops:
  7.2 397.1 %copy-start = (bf16[2048,256]{1,0:T(8,128)(2,1)S(1)}, bf16[2048,256]{1,0:T(8,128)(2,1)}, u32[]{:S(2)}) copy-start(bf16[2048,256]{1,0:T(8,128)(2,1)} %param.13) | copy-start | bytes 3145732
  7.2 72.9 %all-gather.3.cloned.1.call-start = ((), (), s32[]{:S(2)}) async-start(), calls=%async_computation.3 | async-start | bytes 4325376 | tf_op jit(solution)/shard_map/all_gather | solution.py:65
  7.9 250.0 %reduce-scatter.10.cloned.1.call-start = ((), (), s32[]{:S(2)}) async-start(), calls=%async_computation.7 | async-start | bytes 540672
  184.5 169.5 %reduce-scatter.6.cloned.1.call-start = ((), (), s32[]{:S(2)}) async-start(), calls=%async_computation.4 | async-start | bytes 8650752 | tf_op jit(solution)/shard_map/reduce_scatter | solution.py:96
  233.8 170.5 %all-gather.5.cloned.1.call-start = ((), (), s32[]{:S(2)}) async-start(), calls=%async_computation.5 | async-start | bytes 4325376 | tf_op jit(solution)/shard_map/all_gather | solution.py:107
  355.9 73.8 %reduce-scatter.8.cloned.1.call-start = ((), (), s32[]{:S(2)}) async-start(), calls=%async_computation.6 | async-start | bytes 1310720 | tf_op jit(solution)/shard_map/reduce_scatter | solution.py:108
Sparse Core Ops, SparseCore 0:
  10.2 49.8 all-gather.2
  184.6 73.2 reduce-scatter.9
  261.7 92.2 reduce-scatter.5
  356.7 47.5 all-gather.4
  408.9 20.7 reduce-scatter.7
where the time goes:
time: 440 us; the launch traced here: 438 us
  waiting for transfers between devices  189 us (43%)
  other arithmetic  92.6 us (21%)
  matrix products  56 us (13%)
  local copies, waits for them, and re-layouts  44 us (10%)
  blocking collectives  40.4 us (9%)
  between operations  14 us (3%)
    reduce_scatter x1, waiting for transfers between devices, body(): lax.psum_scatter(acc_sum, DP, scatter_dimension=0, tiled=True)  95.3 us
    all_gather x1, waiting for transfers between devices, body(): lax.all_gather(flat_attention, DP, axis=0, tiled=True)  48.4 us
    pmax x3, blocking collectives, one_axis_at_a_time(): return functools.reduce(lax.pmax, axes, array)  40.4 us
    reduce_sum x1, other arithmetic, body(): page_mass = jnp.sum(weights, axis=3)  31.2 us
    reduce_sum x32, other arithmetic, find_owner(): slot_add = jnp.sum(matched * column_numbers[None, None, :], axis=(1, 2))  27.1 us
    unnamed x6, waiting for transfers between devices  24.8 us
    dot_general x2, matrix products, sum_rows(): jnp.dot(onehot_t, flat, preferred_element_type=jnp.float32, precision=lax...  21.6 us
    reduce_scatter x1, waiting for transfers between devices, body(): lax.psum_scatter(partial_value, 'mp', scatter_dimension=0, tiled=True)  20.2 us
  transfers between devices with their start and end apart: 5, of which 4 were waited for; matrix products, arithmetic and copies ran while one was open for 28% of the time, Pallas kernels for 0%

commit v1 on v0

v1 whole, which is shorter than its diff:
```python
import functools

import jax
import jax.numpy as jnp
from jax import lax
from jax.experimental import pallas as pl
from jax.experimental.pallas import tpu as pltpu
from jax.sharding import Mesh
from jax.sharding import PartitionSpec as P

DP = ("dp_0", "dp_1", "dp_2")
MESH = pl.DeviceIdType.MESH
LOW = -1e30
F32 = jnp.float32
BF16 = jnp.bfloat16
NT = (((1,), (1,)), ((), ()))
VMEM = pl.BlockSpec(memory_space=pltpu.VMEM)
SMEM = pl.BlockSpec(memory_space=pltpu.SMEM)
ANY = pl.BlockSpec(memory_space=pl.ANY)


def wrap(value):
    return lax.rem(value + 8, 4)


def place():
    z, y, c = (lax.axis_index(name) for name in DP)
    return z, y, c, 1 - 2 * c


def plane_id(z, y, c):
    return {"dp_0": z, "dp_1": y, "dp_2": c}


def greet(devices):
    barrier = pltpu.get_barrier_semaphore()
    for device in devices:
        pl.semaphore_signal(barrier, inc=1, device_id=device, device_id_type=MESH)
    pl.semaphore_wait(barrier, len(devices))


def remote(src, dst, send_sem, recv_sem, device):
    return pltpu.make_async_remote_copy(
        src_ref=src,
        dst_ref=dst,
        send_sem=send_sem,
        recv_sem=recv_sem,
        device_id=device,
        device_id_type=MESH,
    )


def plane_gather(own, full, ssem, rsem, dsend, drecv, between=()):
    z, y, c, s = place()
    work = list(between)

    def fill():
        if work:
            work.pop(0)()

    def at(h, a, b):
        return full.at[a, b, c, h] if h == 0 else full.at[b, a, c, h]

    def device(h, a, b):
        return plane_id(a, b, c) if h == 0 else plane_id(b, a, c)

    def mine(h):
        return (z, y) if h == 0 else (y, z)

    sent = []

    def go(h, group, m, src, dst, target):
        copy = remote(src, dst, ssem.at[h, group, m], rsem.at[h, group, m], target)
        copy.start()
        sent.append(copy)

    def come(h, group, m, dst):
        remote(dst, dst, ssem.at[h, group, m], rsem.at[h, group, m], plane_id(z, y, c)).wait_recv()

    def share(h, slot, src, dst):
        copy = remote(src, dst, dsend.at[h, slot], drecv.at[h, slot], plane_id(z, y, 1 - c))
        copy.start()
        sent.append(copy)

    def spread(h, group, slot, src, a, b):
        go(h, group, 0, src, at(h, a, b), device(h, mine(h)[0], wrap(b + s)))
        go(h, group, 1, src, at(h, a, b), device(h, mine(h)[0], wrap(b - s)))

    def first(h):
        a, b = mine(h)
        go(h, 0, 0, own.at[h], at(h, a, b), device(h, wrap(a + s), b))
        go(h, 0, 1, own.at[h], at(h, a, b), device(h, wrap(a - s), b))

    for h in range(2):
        first(h)
    for h in range(2):
        share(h, 0, own.at[h], at(h, *mine(h)))
        spread(h, 1, 0, own.at[h], *mine(h))
    fill()
    for h in range(2):
        a, b = mine(h)
        near = wrap(a - s)
        come(h, 0, 0, at(h, near, b))
        go(h, 0, 2, at(h, near, b), at(h, near, b), device(h, wrap(a + s), b))
        spread(h, 2, 4, at(h, near, b), near, b)
        share(h, 4, at(h, near, b), at(h, near, b))
    for h in range(2):
        a, b = mine(h)
        near = wrap(a + s)
        come(h, 0, 1, at(h, near, b))
        spread(h, 3, 8, at(h, near, b), near, b)
        share(h, 8, at(h, near, b), at(h, near, b))
    fill()
    for h in range(2):
        a, b = mine(h)
        far = wrap(a + 2)
        come(h, 0, 2, at(h, far, b))
        spread(h, 4, 12, at(h, far, b), far, b)
        share(h, 12, at(h, far, b), at(h, far, b))
    fill()
    for group, step in ((1, 0), (2, -1), (3, 1), (4, 2)):
        for h in range(2):
            a, b = mine(h)
            row = wrap(a + step * s)
            near = wrap(b - s)
            come(h, group, 0, at(h, row, near))
            go(h, group, 2, at(h, row, near), at(h, row, near), device(h, a, wrap(b + s)))
            share(h, 4 * (group - 1) + 1, at(h, row, near), at(h, row, near))
            other = wrap(b + s)
            come(h, group, 1, at(h, row, other))
            share(h, 4 * (group - 1) + 2, at(h, row, other), at(h, row, other))
        fill()
    for group, step in ((1, 0), (2, -1), (3, 1), (4, 2)):
        for h in range(2):
            a, b = mine(h)
            row = wrap(a + step * s)
            far = wrap(b + 2)
            come(h, group, 2, at(h, row, far))
            share(h, 4 * (group - 1) + 3, at(h, row, far), at(h, row, far))
    for h in range(2):
        for slot in range(16):
            where = full.at[0, 0, 1 - c, h]
            remote(where, where, dsend.at[h, slot], drecv.at[h, slot], plane_id(z, y, 1 - c)).wait_recv()
    return sent


def gather_sems():
    return [
        pltpu.SemaphoreType.DMA((2, 5, 3)),
        pltpu.SemaphoreType.DMA((2, 5, 3)),
        pltpu.SemaphoreType.DMA((2, 16)),
        pltpu.SemaphoreType.DMA((2, 16)),
    ]


def queries_kernel(pool_bits, page_len, q_ref, table_ref, len_ref, full_ref, list_ref, count_ref,
                   lo_ref, hi_ref, part_ref, ssem, rsem, dsend, drecv):
    z, y, c, s = place()
    me = (z * 4 + y) * 2 + c
    greet([plane_id(wrap(z + 1), y, c), plane_id(wrap(z - 1), y, c), plane_id(z, wrap(y + 1), c),
           plane_id(z, wrap(y - 1), c), plane_id(z, y, 1 - c)])
    full_ref[z, y, c] = q_ref[...]

    def place_pages():
        slots = table_ref.shape[0]
        slot = lax.broadcasted_iota(jnp.int32, (slots, 128), 0)
        lane = lax.broadcasted_iota(jnp.int32, (slots, 128), 1)
        blocks = table_ref.shape[1] // 128
        mine, tokens, page, owner = [], [], [], []
        for t in range(blocks):
            ids = table_ref[:, t * 128:(t + 1) * 128]
            length = jnp.broadcast_to(len_ref[t:t + 1, :], (slots, 128))
            left = jnp.clip(length - slot * page_len, 0, page_len)
            mine.append(jnp.where(((ids >> pool_bits) == me) & (left > 0), 1.0, 0.0))
            tokens.append(left)
            page.append(ids & ((1 << pool_bits) - 1))
            owner.append(lane + t * 128)
        mine, tokens, page, owner = (jnp.concatenate(v, axis=0) for v in (mine, tokens, page, owner))
        rows = slots * blocks
        mine_h = mine.astype(BF16)
        i = lax.broadcasted_iota(jnp.int32, (128, 128), 0)
        j = lax.broadcasted_iota(jnp.int32, (128, 128), 1)
        ahead = jnp.where(i < j, 1.0, 0.0).astype(BF16)
        every = jnp.ones((128, 128), BF16)
        within = jnp.dot(mine_h, ahead, preferred_element_type=F32)
        total = jnp.dot(mine_h, every, preferred_element_type=F32)
        i = lax.broadcasted_iota(jnp.int32, (rows, rows), 0)
        j = lax.broadcasted_iota(jnp.int32, (rows, rows), 1)
        before = jnp.where(j < i, 1.0, 0.0).astype(BF16)
        same = jnp.where((j < i) & (i // slots == j // slots), 1.0, 0.0).astype(BF16)
        offset = jnp.dot(before, total.astype(BF16), preferred_element_type=F32)
        earlier = jnp.dot(same, mine_h, preferred_element_type=F32)
        rank = (within + offset).astype(jnp.int32)
        lo_ref[...] = jnp.where(mine > 0.0, rank & 127, -1)
        hi_ref[...] = jnp.where(mine > 0.0, rank >> 7, -1)
        part_ref[0] = (page & 255).astype(F32)
        part_ref[1] = (owner & 255).astype(F32)
        part_ref[2] = ((page >> 8) + ((owner >> 8) << 2) + ((tokens - 1) << 4)).astype(F32)
        part_ref[3] = jnp.where(earlier > 0.0, 0.0, 1.0)
        return (offset + total)[rows - 1:rows, :]

    def make_list():
        count = place_pages()
        rows = lo_ref.shape[0]
        sub = lax.broadcasted_iota(jnp.int32, (128, 128), 0)
        sub8 = lax.broadcasted_iota(jnp.int32, (8, 128), 0)

        def step(n, total):
            base = pl.multiple_of(n * 8, 8)
            lo8 = lo_ref[pl.ds(base, 8), :]
            hi8 = hi_ref[pl.ds(base, 8), :]
            p8 = [part_ref[k, pl.ds(base, 8), :] for k in range(4)]
            wide, tall = [], []
            for r in range(8):
                wide.append(jnp.where(sub == lo8[r:r + 1, :], 1.0, 0.0).astype(BF16))
                hit = sub8 == hi8[r:r + 1, :]
                tall.append(jnp.concatenate(
                    [jnp.where(hit, p8[k][r:r + 1, :], 0.0) for k in range(4)], axis=0).astype(BF16))
            wide = jnp.concatenate(wide, axis=1)
            tall = jnp.concatenate(tall, axis=1)
            return total + lax.dot_general(wide, tall, NT, preferred_element_type=F32)

        total = lax.fori_loop(0, rows // 8, step, jnp.zeros((128, 32), F32))
        total = jnp.concatenate([total, jnp.zeros((128, 96), F32)], axis=1).T.astype(jnp.int32)
        p0, p1, p2, p3 = (total[8 * k:8 * k + 8, :] for k in range(4))
        page = p0 + ((p2 & 3) << 8)
        owner = p1 + (((p2 >> 2) & 3) << 8)
        tokens = (p2 >> 4) + 1
        place_of = sub8 * 128 + lax.broadcasted_iota(jnp.int32, (8, 128), 1)
        number = jnp.broadcast_to(count, (8, 128)).astype(jnp.int32)
        word = page + (owner << 10) + (tokens << 21) + (p3 << 26)
        list_ref[...] = jnp.where(place_of < number, word, (1024 << 10) + (1 << 21) + (1 << 26))
        count_ref[...] = number

    for copy in plane_gather(q_ref, full_ref, ssem, rsem, dsend, drecv, between=(make_list,)):
        copy.wait_send()


def gather_queries(queries, table, lengths, pool, page_len):
    req = table.shape[1]
    rows = table.shape[0] * req // 128
    mine, heads, dim = queries.shape
    half = mine // 2
    return pl.pallas_call(
        functools.partial(queries_kernel, pool.bit_length() - 1, page_len),
        out_shape=(
            jax.ShapeDtypeStruct((4, 4, 2, 2, half, heads, dim), BF16),
            jax.ShapeDtypeStruct((8, 128), jnp.int32),
            jax.ShapeDtypeStruct((8, 128), jnp.int32),
        ),
        in_specs=[VMEM] * 3,
        out_specs=(VMEM, VMEM, VMEM),
        scratch_shapes=[
            pltpu.VMEM((rows, 128), jnp.int32),
            pltpu.VMEM((rows, 128), jnp.int32),
            pltpu.VMEM((4, rows, 128), F32),
        ] + gather_sems(),
        compiler_params=pltpu.CompilerParams(collective_id=0, has_side_effects=True, vmem_limit_bytes=24 << 20),
        name="gather_queries",
    )(queries.reshape(2, half, heads, dim), table, lengths)


def pages_kernel(scale, list_ref, count_ref, q_ref, k_hbm, v_hbm, acc_ref, k_ref, v_ref, m_ref, l_ref, sems):
    pool = k_ref.shape[0]
    chunks = sems.shape[1]
    size = pool // chunks
    loads = []
    for n in range(chunks):
        rows = pl.ds(n * size, size)
        for w, (src, dst) in enumerate(((k_hbm, k_ref), (v_hbm, v_ref))):
            copy = pltpu.make_async_copy(src.at[rows], dst.at[rows], sems.at[w, n])
            copy.start()
            loads.append(copy)
    lane = lax.broadcasted_iota(jnp.int32, (8, 128), 1)
    blank = jnp.where(lane < 32, LOW, 0.0)

    def clear(d, carry):
        for hh in range(2):
            acc_ref[hh, d, 0:32] = jnp.zeros((32, 8, 128), F32)
            acc_ref[hh, d, 32] = blank
        return carry

    lax.fori_loop(0, acc_ref.shape[1], clear, 0)
    for copy in loads:
        copy.wait()

    i = lax.broadcasted_iota(jnp.int32, (16, 128), 0)
    j = lax.broadcasted_iota(jnp.int32, (16, 128), 1)
    kv_match = (i // 8) == (j % 2)
    token = (j % 32) // 2
    token_of = [jnp.where(kv_match & (j // 32 == n), token, 1 << 20) for n in range(4)]

    def step(n, carry):
        base = n * 16
        entries = []
        for e in range(16):
            word = list_ref[(base + e) >> 7, (base + e) & 127]
            entries.append((word & 1023, (word >> 10) & 2047, (word >> 21) & 31, (word >> 26) & 1))
        results = []
        for g in range(4):
            four = entries[4 * g:4 * g + 4]
            qs = jnp.concatenate([q_ref[jnp.minimum(r, 1023)] for _, r, _, _ in four], axis=0)
            ks = jnp.concatenate([k_ref[p] for p, _, _, _ in four], axis=0)
            vs = jnp.concatenate([v_ref[p] for p, _, _, _ in four], axis=0)
            scores = lax.dot_general(qs, ks, NT, preferred_element_type=F32) * scale
            peaks, masses, weights = [], [], []
            for e, (_, _, tokens, _) in enumerate(four):
                valid = token_of[e] < tokens
                sc = jnp.where(valid, scores[16 * e:16 * e + 16], LOW)
                peak = jnp.max(sc, axis=1, keepdims=True)
                w = jnp.where(valid, jnp.exp(sc - peak), 0.0)
                peaks.append(peak)
                masses.append(jnp.sum(w, axis=1, keepdims=True))
                weights.append(w)
            weights = jnp.concatenate(weights, axis=0).astype(BF16)
            out = jnp.dot(weights, vs, preferred_element_type=F32)
            for e in range(4):
                results.append((peaks[e], masses[e], out[16 * e:16 * e + 16]))
        for (_, r, _, first), (peak, mass, out) in zip(entries, results):
            d = r >> 5
            row = r & 31
            fresh = first == 1
            old_m = jnp.where(fresh, LOW, m_ref[r])
            old_l = jnp.where(fresh, 0.0, l_ref[r])
            peak = jnp.broadcast_to(peak, (16, 128))
            new_m = jnp.maximum(old_m, peak)
            f_old = jnp.exp(old_m - new_m)
            f_new = jnp.exp(peak - new_m)
            new_l = old_l * f_old + mass * f_new
            m_ref[r] = new_m
            l_ref[r] = new_l
            pick = (lane == row) | (lane == row + 32)
            for hh in range(2):
                part = slice(8 * hh, 8 * hh + 8)
                acc_ref[hh, d, row] = acc_ref[hh, d, row] * f_old[part] + out[part] * f_new[part]
                both = jnp.where(lane < 32, new_m[part], new_l[part])
                pltpu.store(acc_ref.at[hh, d, 32], both, mask=pick)
        return carry

    lax.fori_loop(0, (count_ref[0, 0] + 15) // 16, step, 0)


def attend_pages(words, count, all_queries, keys, values):
    req, heads, dim = all_queries.shape
    pool = keys.shape[0]
    return pl.pallas_call(
        functools.partial(pages_kernel, dim ** (-0.5)),
        out_shape=jax.ShapeDtypeStruct((2, req // 32 + 1, 33, 8, 128), F32),
        in_specs=[SMEM, SMEM, VMEM, ANY, ANY],
        out_specs=VMEM,
        scratch_shapes=[
            pltpu.VMEM(keys.shape, BF16),
            pltpu.VMEM(keys.shape, BF16),
            pltpu.VMEM((req + 1, heads, dim), F32),
            pltpu.VMEM((req + 1, heads, dim), F32),
            pltpu.SemaphoreType.DMA((2, 8)),
        ],
        compiler_params=pltpu.CompilerParams(vmem_limit_bytes=62 << 20),
        name="attend_pages",
    )(words, count, all_queries, keys, values)


def merge(dst, other):
    lane = lax.broadcasted_iota(jnp.int32, (8, 128), 1)
    t1, t2 = dst[32], other[32]
    top = jnp.maximum(t1, t2)
    f1 = jnp.exp(t1 - top)
    f2 = jnp.exp(t2 - top)
    mass = t1 * pltpu.roll(f1, 32, 1) + t2 * pltpu.roll(f2, 32, 1)
    for row in range(32):
        dst[row] = dst[row] * f1[:, row:row + 1] + other[row] * f2[:, row:row + 1]
    dst[32] = jnp.where(lane < 32, top, mass)


def finish_kernel(part_hbm, w_ref, att_ref, proj_ref, unit, pair, far1, near1, next1, far2, near2, next2,
                  tmp, own, full, cols, farx, nearx, nextx,
                  lsem, s0, r0, s1, r1, s2, r2, ssem, rsem, dsend, drecv, sx, rx):
    z, y, c, s = place()
    x = lax.axis_index("mp")
    home = plane_id(z, y, c)
    greet([plane_id(wrap(z + 1), y, c), plane_id(wrap(z - 1), y, c), plane_id(z, wrap(y + 1), c),
           plane_id(z, wrap(y - 1), c), plane_id(z, y, 1 - c), {"mp": wrap(x + 1)}, {"mp": wrap(x - 1)}])

    def spot(hh, oa, ob):
        dz = oa + hh * (ob - oa)
        dy = ob + hh * (oa - ob)
        return wrap(z + dz), wrap(y + dy)

    def step_of(n):
        m = n % 3
        return 2 * ((3 - n) // 3) + s * (m * (5 - 3 * m) // 2)

    def load(hh, zt, yt):
        return pltpu.make_async_copy(part_hbm.at[hh, (zt * 4 + yt) * 2 + c], unit.at[hh, zt, yt], lsem.at[hh, zt, yt])

    def swap(hh, zt, yt):
        return remote(part_hbm.at[hh, (zt * 4 + yt) * 2 + 1 - c], pair.at[hh, zt, yt], s0.at[hh, zt, yt],
                      r0.at[hh, zt, yt], plane_id(z, y, 1 - c))

    def hop(hh, sign):
        zt, yt = spot(hh, sign * s, 0)
        return plane_id(zt, yt, c)

    def hop2(hh, sign):
        zt, yt = spot(hh, 0, sign * s)
        return plane_id(zt, yt, c)

    order = (0, 2, 1, 3)

    for oa in order:
        def begin(k, carry, oa=oa):
            hh, ob = k % 2, k // 2
            zt, yt = spot(hh, step_of(oa), step_of(ob))
            load(hh, zt, yt).start()
            swap(hh, zt, yt).start()
            return carry
        lax.fori_loop(0, 8, begin, 0)

    def send1(kind, hh, ob, zt, yt):
        dst = (far1, near1, next1)[kind].at[hh, ob]
        return remote(unit.at[hh, zt, yt], dst, s1.at[kind, hh, ob], r1.at[kind, hh, ob], hop(hh, 1 if kind < 2 else -1))

    def both_cores(hh, zt, yt):
        load(hh, zt, yt).wait()
        swap(hh, zt, yt).wait_recv()
        merge(unit.at[hh, zt, yt], pair.at[hh, zt, yt])

    def far_units(k, carry):
        hh, ob = k % 2, k // 2
        zt, yt = spot(hh, 2, step_of(ob))
        both_cores(hh, zt, yt)
        send1(0, hh, ob, zt, yt).start()
        return carry

    def next_units(k, carry):
        hh, ob = k % 2, k // 2
        zt, yt = spot(hh, -s, step_of(ob))
        both_cores(hh, zt, yt)
        send1(2, hh, ob, zt, yt).start()
        return carry

    def near_units(k, carry):
        hh, ob = k % 2, k // 2
        zt, yt = spot(hh, s, step_of(ob))
        both_cores(hh, zt, yt)
        send1(0, hh, ob, zt, yt).wait_recv()
        merge(unit.at[hh, zt, yt], far1.at[hh, ob])
        send1(1, hh, ob, zt, yt).start()
        return carry

    def own_units(k, carry):
        hh, ob = k % 2, k // 2
        zt, yt = spot(hh, 0, step_of(ob))
        both_cores(hh, zt, yt)
        return carry

    lax.fori_loop(0, 8, far_units, 0)
    lax.fori_loop(0, 8, next_units, 0)
    lax.fori_loop(0, 8, near_units, 0)
    lax.fori_loop(0, 8, own_units, 0)

    def send2(kind, hh, zt, yt):
        dst = (far2, near2, next2)[kind].at[hh]
        return remote(unit.at[hh, zt, yt], dst, s2.at[kind, hh], r2.at[kind, hh], hop2(hh, 1 if kind < 2 else -1))

    def gathered(hh, ob):
        zt, yt = spot(hh, 0, step_of(ob))
        send1(2, hh, ob, zt, yt).wait_recv()
        merge(unit.at[hh, zt, yt], next1.at[hh, ob])
        send1(1, hh, ob, zt, yt).wait_recv()
        merge(unit.at[hh, zt, yt], near1.at[hh, ob])
        return zt, yt

    def far_blocks(hh, carry):
        zt, yt = gathered(hh, 0)
        send2(0, hh, zt, yt).start()
        return carry

    def next_blocks(hh, carry):
        zt, yt = gathered(hh, 2)
        send2(2, hh, zt, yt).start()
        return carry

    def near_blocks(hh, carry):
        zt, yt = gathered(hh, 1)
        send2(0, hh, zt, yt).wait_recv()
        merge(unit.at[hh, zt, yt], far2.at[hh])
        send2(1, hh, zt, yt).start()
        return carry

    def own_blocks(hh, carry):
        zt, yt = gathered(hh, 3)
        send2(2, hh, zt, yt).wait_recv()
        merge(unit.at[hh, zt, yt], next2.at[hh])
        send2(1, hh, zt, yt).wait_recv()
        merge(unit.at[hh, zt, yt], near2.at[hh])
        return carry

    for phase in (far_blocks, next_blocks, near_blocks, own_blocks):
        lax.fori_loop(0, 2, phase, 0)

    masses = [unit[hh, z, y, 32] for hh in range(2)]
    for row in range(32):
        both = [unit[hh, z, y, row] / masses[hh][:, 32 + row:33 + row] for hh in range(2)]
        for hh in range(2):
            tmp[hh, row] = both[hh]
        att_ref[row] = jnp.concatenate(both, axis=0).astype(BF16)
    for hh in range(2):
        for head in range(8):
            own[hh, head] = tmp[hh, :, head, :].astype(BF16)
    for hh in range(2):
        full[z, y, c, hh] = own[hh]

    sent = plane_gather(own, full, ssem, rsem, dsend, drecv)

    def project(step):
        t = wrap(x + step)
        rows = [full[t, :, :, hh, head].reshape(256, 128) for hh in range(2) for head in range(8)]
        cols[t] = jnp.dot(jnp.concatenate(rows, axis=1), w_ref[...], preferred_element_type=F32)
        return t

    def sendx(kind, t):
        return remote(cols.at[t], (farx, nearx, nextx)[kind], sx.at[kind], rx.at[kind],
                      {"mp": wrap(x + (s if kind < 2 else -s))})

    t = project(2)
    sendx(0, t).start()
    t = project(-s)
    sendx(2, t).start()
    t = project(s)
    sendx(0, t).wait_recv()
    cols[t] = cols[t] + farx[...]
    sendx(1, t).start()
    t = project(0)
    sendx(2, t).wait_recv()
    total = cols[t] + nextx[...]
    sendx(1, t).wait_recv()
    proj_ref[...] = (total + nearx[...]).astype(BF16)

    for kind in range(3):
        sendx(kind, t).wait_send()
    for copy in sent:
        copy.wait_send()

    def drain(k, carry):
        hh, ob = k % 2, k // 2
        for oa in range(4):
            zt, yt = spot(hh, step_of(oa), step_of(ob))
            swap(hh, zt, yt).wait_send()
        for kind in range(3):
            send1(kind, hh, ob, z, y).wait_send()
        return carry

    lax.fori_loop(0, 8, drain, 0)

    def drain2(hh, carry):
        for kind in range(3):
            send2(kind, hh, z, y).wait_send()
        return carry

    lax.fori_loop(0, 2, drain2, 0)


def finish(parts, weight, rows):
    unit = (33, 8, 128)
    dma = pltpu.SemaphoreType.DMA
    return pl.pallas_call(
        finish_kernel,
        out_shape=(
            jax.ShapeDtypeStruct((rows, 16, 128), BF16),
            jax.ShapeDtypeStruct((256, weight.shape[1]), BF16),
        ),
        in_specs=[ANY, VMEM],
        out_specs=(VMEM, VMEM),
        scratch_shapes=[
            pltpu.VMEM((2, 4, 4) + unit, F32),
            pltpu.VMEM((2, 4, 4) + unit, F32),
            pltpu.VMEM((2, 4) + unit, F32),
            pltpu.VMEM((2, 4) + unit, F32),
            pltpu.VMEM((2, 4) + unit, F32),
            pltpu.VMEM((2,) + unit, F32),
            pltpu.VMEM((2,) + unit, F32),
            pltpu.VMEM((2,) + unit, F32),
            pltpu.VMEM((2, 32, 8, 128), F32),
            pltpu.VMEM((2, 8, 32, 128), BF16),
            pltpu.VMEM((4, 4, 2, 2, 8, 32, 128), BF16),
            pltpu.VMEM((4, 256, 256), F32),
            pltpu.VMEM((256, 256), F32),
            pltpu.VMEM((256, 256), F32),
            pltpu.VMEM((256, 256), F32),
            dma((2, 4, 4)),
            dma((2, 4, 4)),
            dma((2, 4, 4)),
            dma((3, 2, 4)),
            dma((3, 2, 4)),
            dma((3, 2)),
            dma((3, 2)),
        ] + gather_sems() + [dma((3,)), dma((3,))],
        compiler_params=pltpu.CompilerParams(collective_id=1, has_side_effects=True, vmem_limit_bytes=48 << 20),
        name="finish",
    )(parts, weight)


def body(queries, lookup_sheets, content_sheets, page_table, context_len, out_weight):
    req = page_table.shape[0]
    pool, page_len, kv, dim = lookup_sheets.shape
    rows, heads, _ = queries.shape
    all_queries, words, count = gather_queries(
        queries, page_table.T, context_len.reshape(req // 128, 128), pool, page_len
    )
    parts = attend_pages(
        words,
        count,
        all_queries.reshape(req, heads, dim),
        lookup_sheets.reshape(pool, page_len * kv, dim),
        content_sheets.reshape(pool, page_len * kv, dim),
    )
    return finish(parts, out_weight, rows)


def solution(mesh):
    finer = Mesh(mesh.devices.reshape(4, 4, 2, mesh.shape["mp"]), ("dp_0", "dp_1", "dp_2", "mp"))
    return jax.shard_map(
        body,
        mesh=finer,
        in_specs=(
            P(DP, "mp", None),
            P(DP, None, "mp", None),
            P(DP, None, "mp", None),
            P(),
            P(),
            P("mp", DP),
        ),
        out_specs=(P(DP, "mp", None), P("mp", DP)),
        check_vma=False,
    )
```

time: 440 us -> 136 us (0.31)
  waiting for transfers between devices: 189 us -> 0 us
  Pallas kernels: 0 us -> 129 us
  other arithmetic: 92.6 us -> 0 us
  matrix products: 56 us -> 0 us
  blocking collectives: 40.4 us -> 0 us
  local copies, waits for them, and re-layouts: 44 us -> 6.99 us
  between operations: 14 us -> 0.68 us
    pallas_call x0 -> x3, Pallas kernels: none -> 129 us  [the longest x1 68.4 us: finish(): pl.pallas_call(finish_kernel, out_shape=(jax.ShapeDtypeStruct((rows, 16,...]
    reduce_scatter x2 -> x0, waiting for transfers between devices: 115 us -> none  [the longest x1 95.3 us: body(): lax.psum_scatter(acc_sum, DP, scatter_dimension=0, tiled=True)]
    reduce_sum x34 -> x0, other arithmetic: 59.8 us -> none  [the longest x1 31.2 us: body(): page_mass = jnp.sum(weights, axis=3)]
    dot_general x7 -> x0, matrix products: 56 us -> none  [the longest x2 21.6 us: sum_rows(): jnp.dot(onehot_t, flat, preferred_element_type=jnp.float32, precision=lax...]
    all_gather x2 -> x0, waiting for transfers between devices: 48.4 us -> none  [the longest x1 48.4 us: body(): lax.all_gather(flat_attention, DP, axis=0, tiled=True)]
    pmax x3 -> x0, blocking collectives: 40.4 us -> none  [one_axis_at_a_time(): return functools.reduce(lax.pmax, axes, array)]
    unnamed x6 -> x0, waiting for transfers between devices: 24.8 us -> none
    add x96 -> x0, other arithmetic: 20.2 us -> none  [the longest x32 19.8 us: find_owner(): block_start + row_numbers]
  transfers between devices with their start and end apart: 5 -> 0, of which waited for: 4 -> 0; matrix products, arithmetic and copies ran while one was open for 28% -> 0% of each run, Pallas kernels for 0% -> 0%
where the time goes in v1:
time: 136 us
  Pallas kernels  129 us (95%)
  local copies, waits for them, and re-layouts  6.99 us (5%)
    pallas_call x1, Pallas kernels, finish(): pl.pallas_call(finish_kernel, out_shape=(jax.ShapeDtypeStruct((rows, 16,...  68.4 us
    pallas_call x1, Pallas kernels, attend_pages(): pl.pallas_call(functools.partial(pages_kernel, dim ** (-0.5)), out_shape=...  32.5 us
    pallas_call x1, Pallas kernels, gather_queries(): pl.pallas_call(functools.partial(queries_kernel, pool.bit_length() - 1, p...  27.8 us
    unnamed x16, local copies, waits for them, and re-layouts  6.99 us

profile of v1, /device:TPU:1, one launch (start us, length us, event | category | flops | bytes accessed | tf_op | source)
XLA Modules:
  0.0 136.4 jit_solution(15859052626324221354)
XLA Ops:
  0.6 0.0 copy-start.2
  0.6 0.9 copy-done.2
  1.5 0.0 copy-start.3
  1.5 0.9 copy-done.3
  2.4 0.0 copy-start.4
  2.4 0.7 copy-done.4
  3.1 27.8 %gather_queries.1 = (bf16[4,4,2,2,16,16,128]{6,5,4,3,2,1,0:T(8,128)(2,1)S(1)}, s32[8,128]{1,0:T(8,128)S(1)}, s32[8,128]{1,0:T(8,128)S(1)}) custom-call(bf16[2,16,16,128]{3,2,1,0:T(8,128)(2,1)S(1)} %bitcast.7, s32[32,1024]{1,0:T(8,128)S(1)} %bitcast.8, s32[8,128]{1,0:T(8,128)S(1)} %bitcast.9), custom_call_target="tpu_custom_call" | custom-call | tf_op jit(solution)/shard_map/gather_queries/pallas_call | solution.py:244
  30.9 0.0 copy-start
  30.9 2.0 %copy-done = bf16[4,4,2,2,16,16,128]{6,5,4,3,2,1,0:T(8,128)(2,1)} copy-done((bf16[4,4,2,2,16,16,128]{6,5,4,3,2,1,0:T(8,128)(2,1)}, bf16[4,4,2,2,16,16,128]{6,5,4,3,2,1,0:T(8,128)(2,1)S(1)}, u32[]{:S(2)}) %copy-start) | copy-done | bytes 4194328
  32.9 0.0 copy-start.6
  32.9 0.6 copy-done.6
  33.5 0.0 copy-start.5
  33.5 0.6 copy-done.5
  34.1 0.0 copy-start.1
  34.1 32.5 %attend_pages.1.part_hbm = f32[2,33,33,8,128]{4,3,2,1,0:T(8,128)} custom-call(s32[8,128]{1,0:T(8,128)} %copy-done.5, s32[8,128]{1,0:T(8,128)} %copy-done.6, bf16[1024,16,128]{2,1,0:T(8,128)(2,1)} %bitcast.6, bf16[1024,32,128]{2,1,0:T(8,128)(2,1)} %bitcast.10, bf16[1024,32,128]{2,1,0:T(8,128)(2,1)} %bitcast.11), custom_call_target="tpu_custom_call" | custom-call | tf_op jit(solution)/shard_map/attend_pages/pallas_call | solution.py:346
  66.6 0.0 copy-done.1
  66.6 68.4 %finish.1 = (bf16[32,16,128]{2,1,0:T(8,128)(2,1)S(1)}, bf16[256,256]{1,0:T(8,128)(2,1)S(1)}) custom-call(f32[2,33,33,8,128]{4,3,2,1,0:T(8,128)} %attend_pages.1.part_hbm, bf16[2048,256]{1,0:T(8,128)(2,1)S(1)} %copy-done.1), custom_call_target="tpu_custom_call" | custom-call | tf_op jit(solution)/shard_map/finish/pallas_call | solution.py:567
  135.0 0.7 copy.10
  135.7 0.7 copy.11
Async XLA Ops:
  0.6 0.9 copy-start.2
  1.5 0.9 copy-start.3
  2.4 0.7 copy-start.4
  30.9 2.0 %copy-start = (bf16[4,4,2,2,16,16,128]{6,5,4,3,2,1,0:T(8,128)(2,1)}, bf16[4,4,2,2,16,16,128]{6,5,4,3,2,1,0:T(8,128)(2,1)S(1)}, u32[]{:S(2)}) copy-start(bf16[4,4,2,2,16,16,128]{6,5,4,3,2,1,0:T(8,128)(2,1)S(1)} %get-tuple-element.7) | copy-start | bytes 12582916
  32.9 0.6 copy-start.6
  33.5 0.6 copy-start.5
  34.1 32.5 %copy-start.1 = (bf16[2048,256]{1,0:T(8,128)(2,1)S(1)}, bf16[2048,256]{1,0:T(8,128)(2,1)}, u32[]{:S(2)}) copy-start(bf16[2048,256]{1,0:T(8,128)(2,1)} %w_ref.1) | copy-start | bytes 3145732

commit v2 on v1

--- a/solution.py
+++ b/solution.py
@@ -11,12 +11,13 @@
 DP = ("dp_0", "dp_1", "dp_2")
 MESH = pl.DeviceIdType.MESH
 LOW = -1e30
+NOTHING = 1040
 F32 = jnp.float32
 BF16 = jnp.bfloat16
 NT = (((1,), (1,)), ((), ()))
 VMEM = pl.BlockSpec(memory_space=pltpu.VMEM)
+HBM = pl.BlockSpec(memory_space=pltpu.HBM)
 SMEM = pl.BlockSpec(memory_space=pltpu.SMEM)
-ANY = pl.BlockSpec(memory_space=pl.ANY)
 
 
 def wrap(value):
@@ -153,15 +154,24 @@
     ]
 
 
-def queries_kernel(pool_bits, page_len, q_ref, table_ref, len_ref, full_ref, list_ref, count_ref,
-                   lo_ref, hi_ref, part_ref, ssem, rsem, dsend, drecv):
+def queries_kernel(pool_bits, page_len, q_hbm, table_hbm, len_hbm, full_ref, list_ref,
+                   table_ref, len_ref, lo_ref, hi_ref, part_ref, total_ref, lsem, ssem, rsem, dsend, drecv):
     z, y, c, s = place()
     me = (z * 4 + y) * 2 + c
+    loads = [
+        pltpu.make_async_copy(src, dst, lsem.at[n])
+        for n, (src, dst) in enumerate(
+            ((q_hbm, full_ref.at[z, y, c]), (table_hbm, table_ref), (len_hbm, len_ref)))
+    ]
+    for load in loads:
+        load.start()
     greet([plane_id(wrap(z + 1), y, c), plane_id(wrap(z - 1), y, c), plane_id(z, wrap(y + 1), c),
            plane_id(z, wrap(y - 1), c), plane_id(z, y, 1 - c)])
-    full_ref[z, y, c] = q_ref[...]
+    loads[0].wait()
 
     def place_pages():
+        for load in loads[1:]:
+            load.wait()
         slots = table_ref.shape[0]
         slot = lax.broadcasted_iota(jnp.int32, (slots, 128), 0)
         lane = lax.broadcasted_iota(jnp.int32, (slots, 128), 1)
@@ -178,34 +188,40 @@
         mine, tokens, page, owner = (jnp.concatenate(v, axis=0) for v in (mine, tokens, page, owner))
         rows = slots * blocks
         mine_h = mine.astype(BF16)
+        i = lax.broadcasted_iota(jnp.int32, (rows, rows), 0)
+        j = lax.broadcasted_iota(jnp.int32, (rows, rows), 1)
+        same = (i // slots) == (j // slots)
+
+        def count(which, what):
+            return jnp.dot(jnp.where(which, 1.0, 0.0).astype(BF16), what, preferred_element_type=F32)
+
+        earlier = count(same & (j < i), mine_h)
+        column = count(same, mine_h)
+        blocks_before = count((j // slots) < (i // slots), mine_h)
         i = lax.broadcasted_iota(jnp.int32, (128, 128), 0)
         j = lax.broadcasted_iota(jnp.int32, (128, 128), 1)
         ahead = jnp.where(i < j, 1.0, 0.0).astype(BF16)
         every = jnp.ones((128, 128), BF16)
-        within = jnp.dot(mine_h, ahead, preferred_element_type=F32)
-        total = jnp.dot(mine_h, every, preferred_element_type=F32)
-        i = lax.broadcasted_iota(jnp.int32, (rows, rows), 0)
-        j = lax.broadcasted_iota(jnp.int32, (rows, rows), 1)
-        before = jnp.where(j < i, 1.0, 0.0).astype(BF16)
-        same = jnp.where((j < i) & (i // slots == j // slots), 1.0, 0.0).astype(BF16)
-        offset = jnp.dot(before, total.astype(BF16), preferred_element_type=F32)
-        earlier = jnp.dot(same, mine_h, preferred_element_type=F32)
-        rank = (within + offset).astype(jnp.int32)
+        start = jnp.dot(column.astype(BF16), ahead, preferred_element_type=F32)
+        start = start + jnp.dot(blocks_before.astype(BF16), every, preferred_element_type=F32)
+        rank = (start + earlier).astype(jnp.int32)
         lo_ref[...] = jnp.where(mine > 0.0, rank & 127, -1)
         hi_ref[...] = jnp.where(mine > 0.0, rank >> 7, -1)
         part_ref[0] = (page & 255).astype(F32)
         part_ref[1] = (owner & 255).astype(F32)
         part_ref[2] = ((page >> 8) + ((owner >> 8) << 2) + ((tokens - 1) << 4)).astype(F32)
         part_ref[3] = jnp.where(earlier > 0.0, 0.0, 1.0)
-        return (offset + total)[rows - 1:rows, :]
-
-    def make_list():
-        count = place_pages()
-        rows = lo_ref.shape[0]
-        sub = lax.broadcasted_iota(jnp.int32, (128, 128), 0)
-        sub8 = lax.broadcasted_iota(jnp.int32, (8, 128), 0)
-
-        def step(n, total):
+        last = jnp.where(column > 0.0, start + column - 1.0, float(NOTHING)).astype(jnp.int32)
+        list_ref[8:16, :] = jnp.concatenate([last[t * slots:t * slots + 1] for t in range(blocks)], axis=0)
+        number = (start + column)[rows - 1:rows, 127:128]
+        list_ref[16:24, :] = jnp.broadcast_to(number, (8, 128)).astype(jnp.int32)
+        total_ref[...] = jnp.zeros_like(total_ref)
+
+    sub = lax.broadcasted_iota(jnp.int32, (128, 128), 0)
+    sub8 = lax.broadcasted_iota(jnp.int32, (8, 128), 0)
+
+    def scatter(part):
+        def step(n, carry):
             base = pl.multiple_of(n * 8, 8)
             lo8 = lo_ref[pl.ds(base, 8), :]
             hi8 = hi_ref[pl.ds(base, 8), :]
@@ -218,21 +234,22 @@
                     [jnp.where(hit, p8[k][r:r + 1, :], 0.0) for k in range(4)], axis=0).astype(BF16))
             wide = jnp.concatenate(wide, axis=1)
             tall = jnp.concatenate(tall, axis=1)
-            return total + lax.dot_general(wide, tall, NT, preferred_element_type=F32)
-
-        total = lax.fori_loop(0, rows // 8, step, jnp.zeros((128, 32), F32))
-        total = jnp.concatenate([total, jnp.zeros((128, 96), F32)], axis=1).T.astype(jnp.int32)
+            total_ref[...] += lax.dot_general(wide, tall, NT, preferred_element_type=F32)
+            return carry
+
+        steps = lo_ref.shape[0] // 32
+        lax.fori_loop(part * steps, (part + 1) * steps, step, 0)
+
+    def write_list():
+        total = jnp.concatenate([total_ref[...], jnp.zeros((128, 96), F32)], axis=1).T.astype(jnp.int32)
         p0, p1, p2, p3 = (total[8 * k:8 * k + 8, :] for k in range(4))
         page = p0 + ((p2 & 3) << 8)
         owner = p1 + (((p2 >> 2) & 3) << 8)
         tokens = (p2 >> 4) + 1
-        place_of = sub8 * 128 + lax.broadcasted_iota(jnp.int32, (8, 128), 1)
-        number = jnp.broadcast_to(count, (8, 128)).astype(jnp.int32)
-        word = page + (owner << 10) + (tokens << 21) + (p3 << 26)
-        list_ref[...] = jnp.where(place_of < number, word, (1024 << 10) + (1 << 21) + (1 << 26))
-        count_ref[...] = number
-
-    for copy in plane_gather(q_ref, full_ref, ssem, rsem, dsend, drecv, between=(make_list,)):
+        list_ref[0:8, :] = page + (owner << 10) + (tokens << 20) + (p3 << 25)
+
+    pieces = [place_pages] + [functools.partial(scatter, n) for n in range(4)] + [write_list]
+    for copy in plane_gather(full_ref.at[z, y, c], full_ref, ssem, rsem, dsend, drecv, between=pieces):
         copy.wait_send()
 
 
@@ -245,61 +262,46 @@
         functools.partial(queries_kernel, pool.bit_length() - 1, page_len),
         out_shape=(
             jax.ShapeDtypeStruct((4, 4, 2, 2, half, heads, dim), BF16),
-            jax.ShapeDtypeStruct((8, 128), jnp.int32),
-            jax.ShapeDtypeStruct((8, 128), jnp.int32),
+            jax.ShapeDtypeStruct((24, 128), jnp.int32),
         ),
-        in_specs=[VMEM] * 3,
-        out_specs=(VMEM, VMEM, VMEM),
+        in_specs=[HBM] * 3,
+        out_specs=(VMEM, VMEM),
         scratch_shapes=[
+            pltpu.VMEM(table.shape, jnp.int32),
+            pltpu.VMEM(lengths.shape, jnp.int32),
             pltpu.VMEM((rows, 128), jnp.int32),
             pltpu.VMEM((rows, 128), jnp.int32),
             pltpu.VMEM((4, rows, 128), F32),
+            pltpu.VMEM((128, 32), F32),
+            pltpu.SemaphoreType.DMA((3,)),
         ] + gather_sems(),
-        compiler_params=pltpu.CompilerParams(collective_id=0, has_side_effects=True, vmem_limit_bytes=24 << 20),
+        compiler_params=pltpu.CompilerParams(collective_id=0, has_side_effects=True, vmem_limit_bytes=8 << 20),
+        cost_estimate=pl.CostEstimate(flops=10**10, bytes_accessed=1 << 23, transcendentals=0),
         name="gather_queries",
     )(queries.reshape(2, half, heads, dim), table, lengths)
 
 
-def pages_kernel(scale, list_ref, count_ref, q_ref, k_hbm, v_hbm, acc_ref, k_ref, v_ref, m_ref, l_ref, sems):
-    pool = k_ref.shape[0]
-    chunks = sems.shape[1]
-    size = pool // chunks
-    loads = []
-    for n in range(chunks):
-        rows = pl.ds(n * size, size)
-        for w, (src, dst) in enumerate(((k_hbm, k_ref), (v_hbm, v_ref))):
-            copy = pltpu.make_async_copy(src.at[rows], dst.at[rows], sems.at[w, n])
-            copy.start()
-            loads.append(copy)
-    lane = lax.broadcasted_iota(jnp.int32, (8, 128), 1)
+def pages_kernel(scale, list_ref, q_ref, k_ref, v_ref, acc_ref, sum_ref, top_ref):
+    lane = lax.broadcasted_iota(jnp.int32, (16, 128), 1)
     blank = jnp.where(lane < 32, LOW, 0.0)
-
-    def clear(d, carry):
-        for hh in range(2):
-            acc_ref[hh, d, 0:32] = jnp.zeros((32, 8, 128), F32)
-            acc_ref[hh, d, 32] = blank
-        return carry
-
-    lax.fori_loop(0, acc_ref.shape[1], clear, 0)
-    for copy in loads:
-        copy.wait()
+    sum_ref[NOTHING] = jnp.zeros((16, 128), F32)
+    top_ref[NOTHING] = blank
 
     i = lax.broadcasted_iota(jnp.int32, (16, 128), 0)
-    j = lax.broadcasted_iota(jnp.int32, (16, 128), 1)
-    kv_match = (i // 8) == (j % 2)
-    token = (j % 32) // 2
-    token_of = [jnp.where(kv_match & (j // 32 == n), token, 1 << 20) for n in range(4)]
+    kv_match = (i // 8) == (lane % 2)
+    token = (lane % 32) // 2
+    token_of = [jnp.where(kv_match & (lane // 32 == n), token, 1 << 20) for n in range(4)]
 
     def step(n, carry):
         base = n * 16
         entries = []
         for e in range(16):
             word = list_ref[(base + e) >> 7, (base + e) & 127]
-            entries.append((word & 1023, (word >> 10) & 2047, (word >> 21) & 31, (word >> 26) & 1))
+            entries.append((word & 1023, (word >> 10) & 1023, (word >> 20) & 31, (word >> 25) & 1))
         results = []
         for g in range(4):
             four = entries[4 * g:4 * g + 4]
-            qs = jnp.concatenate([q_ref[jnp.minimum(r, 1023)] for _, r, _, _ in four], axis=0)
+            qs = jnp.concatenate([q_ref[r] for _, r, _, _ in four], axis=0)
             ks = jnp.concatenate([k_ref[p] for p, _, _, _ in four], axis=0)
             vs = jnp.concatenate([v_ref[p] for p, _, _, _ in four], axis=0)
             scores = lax.dot_general(qs, ks, NT, preferred_element_type=F32) * scale
@@ -316,65 +318,69 @@
             out = jnp.dot(weights, vs, preferred_element_type=F32)
             for e in range(4):
                 results.append((peaks[e], masses[e], out[16 * e:16 * e + 16]))
-        for (_, r, _, first), (peak, mass, out) in zip(entries, results):
-            d = r >> 5
-            row = r & 31
-            fresh = first == 1
-            old_m = jnp.where(fresh, LOW, m_ref[r])
-            old_l = jnp.where(fresh, 0.0, l_ref[r])
-            peak = jnp.broadcast_to(peak, (16, 128))
-            new_m = jnp.maximum(old_m, peak)
-            f_old = jnp.exp(old_m - new_m)
-            f_new = jnp.exp(peak - new_m)
-            new_l = old_l * f_old + mass * f_new
-            m_ref[r] = new_m
-            l_ref[r] = new_l
-            pick = (lane == row) | (lane == row + 32)
+        top, mass, acc = carry
+        for e, ((_, _, _, first), (p, m, out)) in enumerate(zip(entries, results)):
+            old = jnp.where(first == 1, LOW, top)
+            p = jnp.broadcast_to(p, (16, 128))
+            top = jnp.maximum(old, p)
+            f_old = jnp.exp(old - top)
+            f_new = jnp.exp(p - top)
+            mass = mass * f_old + m * f_new
+            acc = acc * f_old + out * f_new
+            sum_ref[base + e] = acc
+            top_ref[base + e] = jnp.where(lane < 32, top, mass)
+        return top, mass, acc
+
+    zero = jnp.zeros((16, 128), F32)
+    lax.fori_loop(0, (list_ref[16, 0] + 15) // 16, step, (zero, zero, zero))
+
+    def spread(d, carry):
+        tops = blank
+        for row in range(32):
+            r = d * 32 + row
+            last = list_ref[8 + (r >> 7), r & 127]
+            acc = sum_ref[last]
+            tops = jnp.where((lane == row) | (lane == row + 32), top_ref[last], tops)
             for hh in range(2):
-                part = slice(8 * hh, 8 * hh + 8)
-                acc_ref[hh, d, row] = acc_ref[hh, d, row] * f_old[part] + out[part] * f_new[part]
-                both = jnp.where(lane < 32, new_m[part], new_l[part])
-                pltpu.store(acc_ref.at[hh, d, 32], both, mask=pick)
-        return carry
-
-    lax.fori_loop(0, (count_ref[0, 0] + 15) // 16, step, 0)
-
-
-def attend_pages(words, count, all_queries, keys, values):
+                acc_ref[hh, d, row] = acc[8 * hh:8 * hh + 8]
+        for hh in range(2):
+            acc_ref[hh, d, 32] = tops[8 * hh:8 * hh + 8]
+        return carry
+
+    lax.fori_loop(0, acc_ref.shape[1], spread, 0)
+
+
+def attend_pages(words, all_queries, keys, values):
     req, heads, dim = all_queries.shape
-    pool = keys.shape[0]
     return pl.pallas_call(
         functools.partial(pages_kernel, dim ** (-0.5)),
-        out_shape=jax.ShapeDtypeStruct((2, req // 32 + 1, 33, 8, 128), F32),
-        in_specs=[SMEM, SMEM, VMEM, ANY, ANY],
+        out_shape=jax.ShapeDtypeStruct((2, req // 32, 33, 8, 128), F32),
+        in_specs=[SMEM, VMEM, VMEM, VMEM],
         out_specs=VMEM,
         scratch_shapes=[
-            pltpu.VMEM(keys.shape, BF16),
-            pltpu.VMEM(keys.shape, BF16),
-            pltpu.VMEM((req + 1, heads, dim), F32),
-            pltpu.VMEM((req + 1, heads, dim), F32),
-            pltpu.SemaphoreType.DMA((2, 8)),
+            pltpu.VMEM((NOTHING + 1, heads, dim), F32),
+            pltpu.VMEM((NOTHING + 1, heads, dim), F32),
         ],
-        compiler_params=pltpu.CompilerParams(vmem_limit_bytes=62 << 20),
+        compiler_params=pltpu.CompilerParams(vmem_limit_bytes=20 << 20),
         name="attend_pages",
-    )(words, count, all_queries, keys, values)
-
-
-def merge(dst, other):
+    )(words, all_queries, keys, values)
+
+
+def merge(dst, one, other):
     lane = lax.broadcasted_iota(jnp.int32, (8, 128), 1)
-    t1, t2 = dst[32], other[32]
+    t1, t2 = one[32], other[32]
     top = jnp.maximum(t1, t2)
     f1 = jnp.exp(t1 - top)
     f2 = jnp.exp(t2 - top)
     mass = t1 * pltpu.roll(f1, 32, 1) + t2 * pltpu.roll(f2, 32, 1)
     for row in range(32):
-        dst[row] = dst[row] * f1[:, row:row + 1] + other[row] * f2[:, row:row + 1]
+        dst[row] = one[row] * f1[:, row:row + 1] + other[row] * f2[:, row:row + 1]
     dst[32] = jnp.where(lane < 32, top, mass)
 
 
-def finish_kernel(part_hbm, w_ref, att_ref, proj_ref, unit, pair, far1, near1, next1, far2, near2, next2,
+def finish_kernel(part_ref, w_ref, att_ref, proj_ref, unit, pair, far1, near1, next1, far2, near2, next2,
                   tmp, own, full, cols, farx, nearx, nextx,
-                  lsem, s0, r0, s1, r1, s2, r2, ssem, rsem, dsend, drecv, sx, rx):
+                  s0, r0, s1, r1, s2, r2, ssem, rsem, dsend, drecv, sx, rx):
     z, y, c, s = place()
     x = lax.axis_index("mp")
     home = plane_id(z, y, c)
@@ -390,11 +396,8 @@
         m = n % 3
         return 2 * ((3 - n) // 3) + s * (m * (5 - 3 * m) // 2)
 
-    def load(hh, zt, yt):
-        return pltpu.make_async_copy(part_hbm.at[hh, (zt * 4 + yt) * 2 + c], unit.at[hh, zt, yt], lsem.at[hh, zt, yt])
-
     def swap(hh, zt, yt):
-        return remote(part_hbm.at[hh, (zt * 4 + yt) * 2 + 1 - c], pair.at[hh, zt, yt], s0.at[hh, zt, yt],
+        return remote(part_ref.at[hh, (zt * 4 + yt) * 2 + 1 - c], pair.at[hh, zt, yt], s0.at[hh, zt, yt],
                       r0.at[hh, zt, yt], plane_id(z, y, 1 - c))
 
     def hop(hh, sign):
@@ -411,7 +414,6 @@
         def begin(k, carry, oa=oa):
             hh, ob = k % 2, k // 2
             zt, yt = spot(hh, step_of(oa), step_of(ob))
-            load(hh, zt, yt).start()
             swap(hh, zt, yt).start()
             return carry
         lax.fori_loop(0, 8, begin, 0)
@@ -421,9 +423,8 @@
         return remote(unit.at[hh, zt, yt], dst, s1.at[kind, hh, ob], r1.at[kind, hh, ob], hop(hh, 1 if kind < 2 else -1))
 
     def both_cores(hh, zt, yt):
-        load(hh, zt, yt).wait()
         swap(hh, zt, yt).wait_recv()
-        merge(unit.at[hh, zt, yt], pair.at[hh, zt, yt])
+        merge(unit.at[hh, zt, yt], part_ref.at[hh, (zt * 4 + yt) * 2 + c], pair.at[hh, zt, yt])
 
     def far_units(k, carry):
         hh, ob = k % 2, k // 2
@@ -444,7 +445,7 @@
         zt, yt = spot(hh, s, step_of(ob))
         both_cores(hh, zt, yt)
         send1(0, hh, ob, zt, yt).wait_recv()
-        merge(unit.at[hh, zt, yt], far1.at[hh, ob])
+        merge(unit.at[hh, zt, yt], unit.at[hh, zt, yt], far1.at[hh, ob])
         send1(1, hh, ob, zt, yt).start()
         return carry
 
@@ -466,9 +467,9 @@
     def gathered(hh, ob):
         zt, yt = spot(hh, 0, step_of(ob))
         send1(2, hh, ob, zt, yt).wait_recv()
-        merge(unit.at[hh, zt, yt], next1.at[hh, ob])
+        merge(unit.at[hh, zt, yt], unit.at[hh, zt, yt], next1.at[hh, ob])
         send1(1, hh, ob, zt, yt).wait_recv()
-        merge(unit.at[hh, zt, yt], near1.at[hh, ob])
+        merge(unit.at[hh, zt, yt], unit.at[hh, zt, yt], near1.at[hh, ob])
         return zt, yt
 
     def far_blocks(hh, carry):
@@ -484,16 +485,16 @@
     def near_blocks(hh, carry):
         zt, yt = gathered(hh, 1)
         send2(0, hh, zt, yt).wait_recv()
-        merge(unit.at[hh, zt, yt], far2.at[hh])
+        merge(unit.at[hh, zt, yt], unit.at[hh, zt, yt], far2.at[hh])
         send2(1, hh, zt, yt).start()
         return carry
 
     def own_blocks(hh, carry):
         zt, yt = gathered(hh, 3)
         send2(2, hh, zt, yt).wait_recv()
-        merge(unit.at[hh, zt, yt], next2.at[hh])
+        merge(unit.at[hh, zt, yt], unit.at[hh, zt, yt], next2.at[hh])
         send2(1, hh, zt, yt).wait_recv()
-        merge(unit.at[hh, zt, yt], near2.at[hh])
+        merge(unit.at[hh, zt, yt], unit.at[hh, zt, yt], near2.at[hh])
         return carry
 
     for phase in (far_blocks, next_blocks, near_blocks, own_blocks):
@@ -570,7 +571,7 @@
             jax.ShapeDtypeStruct((rows, 16, 128), BF16),
             jax.ShapeDtypeStruct((256, weight.shape[1]), BF16),
         ),
-        in_specs=[ANY, VMEM],
+        in_specs=[VMEM, VMEM],
         out_specs=(VMEM, VMEM),
         scratch_shapes=[
             pltpu.VMEM((2, 4, 4) + unit, F32),
@@ -590,13 +591,12 @@
             pltpu.VMEM((256, 256), F32),
             dma((2, 4, 4)),
             dma((2, 4, 4)),
-            dma((2, 4, 4)),
             dma((3, 2, 4)),
             dma((3, 2, 4)),
             dma((3, 2)),
             dma((3, 2)),
         ] + gather_sems() + [dma((3,)), dma((3,))],
-        compiler_params=pltpu.CompilerParams(collective_id=1, has_side_effects=True, vmem_limit_bytes=48 << 20),
+        compiler_params=pltpu.CompilerParams(collective_id=1, has_side_effects=True, vmem_limit_bytes=24 << 20),
         name="finish",
     )(parts, weight)
 
@@ -605,12 +605,11 @@
     req = page_table.shape[0]
     pool, page_len, kv, dim = lookup_sheets.shape
     rows, heads, _ = queries.shape
-    all_queries, words, count = gather_queries(
+    all_queries, words = gather_queries(
         queries, page_table.T, context_len.reshape(req // 128, 128), pool, page_len
     )
     parts = attend_pages(
         words,
-        count,
         all_queries.reshape(req, heads, dim),
         lookup_sheets.reshape(pool, page_len * kv, dim),
         content_sheets.reshape(pool, page_len * kv, dim),

time: 136 us -> 123 us (0.904)
  Pallas kernels: 129 us -> 118 us
  local copies, waits for them, and re-layouts: 6.99 us -> 3.81 us
    pallas_call x1, Pallas kernels: 32.5 us -> 26.7 us  [attend_pages(): pl.pallas_call(functools.partial(pages_kernel, dim ** (-0.5)), out_shape=...]
    pallas_call x1, Pallas kernels: 68.4 us -> 64.5 us  [finish(): pl.pallas_call(finish_kernel, out_shape=(jax.ShapeDtypeStruct((rows, 16,...]
    unnamed x16 -> x14, local copies, waits for them, and re-layouts: 6.99 us -> 3.81 us
where the time goes in v2:
time: 123 us
  Pallas kernels  118 us (96%)
  local copies, waits for them, and re-layouts  3.81 us (3%)
    pallas_call x1, Pallas kernels, finish(): pl.pallas_call(finish_kernel, out_shape=(jax.ShapeDtypeStruct((rows, 16,...  64.5 us
    pallas_call x1, Pallas kernels, gather_queries(): pl.pallas_call(functools.partial(queries_kernel, pool.bit_length() - 1, p...  27.1 us
    pallas_call x1, Pallas kernels, attend_pages(): pl.pallas_call(functools.partial(pages_kernel, dim ** (-0.5)), out_shape=...  26.7 us
    unnamed x14, local copies, waits for them, and re-layouts  3.81 us

profile of v2, /device:TPU:1, one launch (start us, length us, event | category | flops | bytes accessed | tf_op | source)
XLA Modules:
  0.0 122.8 jit_solution(9347329817220584235)
XLA Ops:
  0.6 0.0 copy-start.3
  0.6 0.9 copy-done.3
  1.5 0.0 copy-start.4
  1.5 0.9 copy-done.4
  2.4 0.0 copy-start.5
  2.4 0.7 copy-done.5
  3.1 0.0 copy-start
  3.1 0.0 copy-start.1
  3.1 27.1 %gather_queries.1 = (bf16[4,4,2,2,16,16,128]{6,5,4,3,2,1,0:T(8,128)(2,1)S(1)}, s32[24,128]{1,0:T(8,128)S(1)}) custom-call(bf16[2,16,16,128]{3,2,1,0:T(8,128)(2,1)S(1)} %bitcast.9, s32[32,1024]{1,0:T(8,128)S(1)} %bitcast.10, s32[8,128]{1,0:T(8,128)S(1)} %bitcast.11), custom_call_target="tpu_custom_call" | custom-call | flops 10000000000 | bytes 8388608 | tf_op jit(solution)/shard_map/gather_queries/pallas_call | solution.py:261
  30.2 0.0 copy-done
  30.2 0.0 copy-done.1
  30.2 0.0 copy-start.2
  30.2 26.7 %attend_pages.1.part_ref = f32[2,32,33,8,128]{4,3,2,1,0:T(8,128)S(1)} custom-call(s32[24,128]{1,0:T(8,128)S(1)} %get-tuple-element.4.list_ref, bf16[1024,16,128]{2,1,0:T(8,128)(2,1)S(1)} %bitcast.8, bf16[1024,32,128]{2,1,0:T(8,128)(2,1)S(1)} %bitcast.6, bf16[1024,32,128]{2,1,0:T(8,128)(2,1)S(1)} %bitcast.7), custom_call_target="tpu_custom_call" | custom-call | tf_op jit(solution)/shard_map/attend_pages/pallas_call | solution.py:355
  57.0 0.0 copy-done.2
  57.0 64.5 %finish.1 = (bf16[32,16,128]{2,1,0:T(8,128)(2,1)S(1)}, bf16[256,256]{1,0:T(8,128)(2,1)S(1)}) custom-call(f32[2,32,33,8,128]{4,3,2,1,0:T(8,128)S(1)} %attend_pages.1.part_ref, bf16[2048,256]{1,0:T(8,128)(2,1)S(1)} %copy-done.2), custom_call_target="tpu_custom_call" | custom-call | tf_op jit(solution)/shard_map/finish/pallas_call | solution.py:568
  121.5 0.7 copy.10
  122.2 0.7 copy.11
Async XLA Ops:
  0.6 0.9 copy-start.3
  1.5 0.9 copy-start.4
  2.4 0.7 copy-start.5
  3.1 27.1 %copy-start = (bf16[1024,16,2,128]{3,2,1,0:T(2,128)(2,1)S(1)}, bf16[1024,16,2,128]{3,2,1,0:T(2,128)(2,1)}, u32[]{:S(2)}) copy-start(bf16[1024,16,2,128]{3,2,1,0:T(2,128)(2,1)} %param.7) | copy-start | bytes 25165828
  3.1 27.1 %copy-start.1 = (bf16[1024,16,2,128]{3,2,1,0:T(2,128)(2,1)S(1)}, bf16[1024,16,2,128]{3,2,1,0:T(2,128)(2,1)}, u32[]{:S(2)}) copy-start(bf16[1024,16,2,128]{3,2,1,0:T(2,128)(2,1)} %param.8) | copy-start | bytes 25165828
  30.2 26.8 %copy-start.2 = (bf16[2048,256]{1,0:T(8,128)(2,1)S(1)}, bf16[2048,256]{1,0:T(8,128)(2,1)}, u32[]{:S(2)}) copy-start(bf16[2048,256]{1,0:T(8,128)(2,1)} %w_ref.1) | copy-start | bytes 3145732

commit v3 on v2

--- a/solution.py
+++ b/solution.py
@@ -11,7 +11,8 @@
 DP = ("dp_0", "dp_1", "dp_2")
 MESH = pl.DeviceIdType.MESH
 LOW = -1e30
-NOTHING = 1040
+BATCH = 32
+NOTHING = 1056
 F32 = jnp.float32
 BF16 = jnp.bfloat16
 NT = (((1,), (1,)), ((), ()))
@@ -91,6 +92,7 @@
         a, b = mine(h)
         go(h, 0, 0, own.at[h], at(h, a, b), device(h, wrap(a + s), b))
         go(h, 0, 1, own.at[h], at(h, a, b), device(h, wrap(a - s), b))
+        go(h, 0, 2, own.at[h], at(h, a, b), device(h, wrap(a + 2), b))
 
     for h in range(2):
         first(h)
@@ -102,7 +104,6 @@
         a, b = mine(h)
         near = wrap(a - s)
         come(h, 0, 0, at(h, near, b))
-        go(h, 0, 2, at(h, near, b), at(h, near, b), device(h, wrap(a + s), b))
         spread(h, 2, 4, at(h, near, b), near, b)
         share(h, 4, at(h, near, b), at(h, near, b))
     for h in range(2):
@@ -166,7 +167,7 @@
     for load in loads:
         load.start()
     greet([plane_id(wrap(z + 1), y, c), plane_id(wrap(z - 1), y, c), plane_id(z, wrap(y + 1), c),
-           plane_id(z, wrap(y - 1), c), plane_id(z, y, 1 - c)])
+           plane_id(z, wrap(y - 1), c), plane_id(wrap(z + 2), y, c), plane_id(z, wrap(y + 2), c), plane_id(z, y, 1 - c)])
     loads[0].wait()
 
     def place_pages():
@@ -256,8 +257,7 @@
 def gather_queries(queries, table, lengths, pool, page_len):
     req = table.shape[1]
     rows = table.shape[0] * req // 128
-    mine, heads, dim = queries.shape
-    half = mine // 2
+    _, half, heads, dim = queries.shape
     return pl.pallas_call(
         functools.partial(queries_kernel, pool.bit_length() - 1, page_len),
         out_shape=(
@@ -278,61 +278,67 @@
         compiler_params=pltpu.CompilerParams(collective_id=0, has_side_effects=True, vmem_limit_bytes=8 << 20),
         cost_estimate=pl.CostEstimate(flops=10**10, bytes_accessed=1 << 23, transcendentals=0),
         name="gather_queries",
-    )(queries.reshape(2, half, heads, dim), table, lengths)
-
-
-def pages_kernel(scale, list_ref, q_ref, k_ref, v_ref, acc_ref, sum_ref, top_ref):
+    )(queries, table, lengths)
+
+
+def pages_kernel(scale, list_ref, q_ref, k_ref, v_ref, acc_ref, sum_ref, top_ref, wait_ref, peak_ref, mass_ref):
     lane = lax.broadcasted_iota(jnp.int32, (16, 128), 1)
     blank = jnp.where(lane < 32, LOW, 0.0)
-    sum_ref[NOTHING] = jnp.zeros((16, 128), F32)
+    zero = jnp.zeros((16, 128), F32)
+    sum_ref[NOTHING] = zero
     top_ref[NOTHING] = blank
+    wait_ref[...] = jnp.zeros_like(wait_ref)
+    peak_ref[...] = jnp.zeros_like(peak_ref)
+    mass_ref[...] = jnp.zeros_like(mass_ref)
 
     i = lax.broadcasted_iota(jnp.int32, (16, 128), 0)
     kv_match = (i // 8) == (lane % 2)
     token = (lane % 32) // 2
     token_of = [jnp.where(kv_match & (lane // 32 == n), token, 1 << 20) for n in range(4)]
 
+    def entry(k):
+        word = list_ref[k >> 7, k & 127]
+        return word & 1023, (word >> 10) & 1023, (word >> 20) & 31, (word >> 25) & 1
+
     def step(n, carry):
-        base = n * 16
-        entries = []
-        for e in range(16):
-            word = list_ref[(base + e) >> 7, (base + e) & 127]
-            entries.append((word & 1023, (word >> 10) & 1023, (word >> 20) & 31, (word >> 25) & 1))
-        results = []
-        for g in range(4):
-            four = entries[4 * g:4 * g + 4]
-            qs = jnp.concatenate([q_ref[r] for _, r, _, _ in four], axis=0)
-            ks = jnp.concatenate([k_ref[p] for p, _, _, _ in four], axis=0)
-            vs = jnp.concatenate([v_ref[p] for p, _, _, _ in four], axis=0)
-            scores = lax.dot_general(qs, ks, NT, preferred_element_type=F32) * scale
-            peaks, masses, weights = [], [], []
-            for e, (_, _, tokens, _) in enumerate(four):
-                valid = token_of[e] < tokens
-                sc = jnp.where(valid, scores[16 * e:16 * e + 16], LOW)
-                peak = jnp.max(sc, axis=1, keepdims=True)
-                w = jnp.where(valid, jnp.exp(sc - peak), 0.0)
-                peaks.append(peak)
-                masses.append(jnp.sum(w, axis=1, keepdims=True))
-                weights.append(w)
-            weights = jnp.concatenate(weights, axis=0).astype(BF16)
-            out = jnp.dot(weights, vs, preferred_element_type=F32)
-            for e in range(4):
-                results.append((peaks[e], masses[e], out[16 * e:16 * e + 16]))
+        past = jnp.maximum(n - 1, 0) * BATCH
+        base = n * BATCH
+        before = [entry(past + e) for e in range(BATCH)]
+        now = [entry(base + e) for e in range(BATCH)]
+        outs, scores = [], []
+        for g in range(BATCH // 4):
+            four = slice(4 * g, 4 * g + 4)
+            vs = jnp.concatenate([v_ref[p] for p, _, _, _ in before[four]], axis=0)
+            outs.append(jnp.dot(wait_ref[g], vs, preferred_element_type=F32))
+            qs = jnp.concatenate([q_ref[r] for _, r, _, _ in now[four]], axis=0)
+            ks = jnp.concatenate([k_ref[p] for p, _, _, _ in now[four]], axis=0)
+            scores.append(lax.dot_general(qs, ks, NT, preferred_element_type=F32))
         top, mass, acc = carry
-        for e, ((_, _, _, first), (p, m, out)) in enumerate(zip(entries, results)):
+        for e, (_, _, _, first) in enumerate(before):
             old = jnp.where(first == 1, LOW, top)
-            p = jnp.broadcast_to(p, (16, 128))
+            p = peak_ref[e]
             top = jnp.maximum(old, p)
             f_old = jnp.exp(old - top)
             f_new = jnp.exp(p - top)
-            mass = mass * f_old + m * f_new
-            acc = acc * f_old + out * f_new
-            sum_ref[base + e] = acc
-            top_ref[base + e] = jnp.where(lane < 32, top, mass)
+            mass = mass * f_old + mass_ref[e] * f_new
+            acc = acc * f_old + outs[e // 4][16 * (e % 4):16 * (e % 4) + 16] * f_new
+            sum_ref[past + e] = acc
+            top_ref[past + e] = jnp.where(lane < 32, top, mass)
+        for g in range(BATCH // 4):
+            weights = []
+            for e in range(4):
+                valid = token_of[e] < now[4 * g + e][2]
+                sc = jnp.where(valid, scores[g][16 * e:16 * e + 16] * scale, LOW)
+                peak = jnp.max(sc, axis=1, keepdims=True)
+                w = jnp.where(valid, jnp.exp(sc - peak), 0.0)
+                peak_ref[4 * g + e] = jnp.broadcast_to(peak, (16, 128))
+                mass_ref[4 * g + e] = jnp.broadcast_to(jnp.sum(w, axis=1, keepdims=True), (16, 128))
+                weights.append(w)
+            wait_ref[g] = jnp.concatenate(weights, axis=0).astype(BF16)
         return top, mass, acc
 
-    zero = jnp.zeros((16, 128), F32)
-    lax.fori_loop(0, (list_ref[16, 0] + 15) // 16, step, (zero, zero, zero))
+    batches = (list_ref[16, 0] + BATCH - 1) // BATCH
+    lax.fori_loop(0, batches + 1, step, (zero, zero, zero))
 
     def spread(d, carry):
         tops = blank
@@ -360,6 +366,9 @@
         scratch_shapes=[
             pltpu.VMEM((NOTHING + 1, heads, dim), F32),
             pltpu.VMEM((NOTHING + 1, heads, dim), F32),
+            pltpu.VMEM((BATCH // 4, 4 * heads, dim), BF16),
+            pltpu.VMEM((BATCH, heads, dim), F32),
+            pltpu.VMEM((BATCH, heads, dim), F32),
         ],
         compiler_params=pltpu.CompilerParams(vmem_limit_bytes=20 << 20),
         name="attend_pages",
@@ -385,7 +394,7 @@
     x = lax.axis_index("mp")
     home = plane_id(z, y, c)
     greet([plane_id(wrap(z + 1), y, c), plane_id(wrap(z - 1), y, c), plane_id(z, wrap(y + 1), c),
-           plane_id(z, wrap(y - 1), c), plane_id(z, y, 1 - c), {"mp": wrap(x + 1)}, {"mp": wrap(x - 1)}])
+           plane_id(z, wrap(y - 1), c), plane_id(wrap(z + 2), y, c), plane_id(z, wrap(y + 2), c), plane_id(z, y, 1 - c), {"mp": wrap(x + 1)}, {"mp": wrap(x - 1)}])
 
     def spot(hh, oa, ob):
         dz = oa + hh * (ob - oa)
@@ -606,7 +615,10 @@
     pool, page_len, kv, dim = lookup_sheets.shape
     rows, heads, _ = queries.shape
     all_queries, words = gather_queries(
-        queries, page_table.T, context_len.reshape(req // 128, 128), pool, page_len
+        *(pltpu.with_memory_space_constraint(a, pltpu.HBM)
+          for a in (queries.reshape(2, rows // 2, heads, dim), page_table.T, context_len.reshape(req // 128, 128))),
+        pool,
+        page_len,
     )
     parts = attend_pages(
         words,

time: 123 us -> 103 us (0.84)
  Pallas kernels: 118 us -> 101 us
  local copies, waits for them, and re-layouts: 3.81 us -> 1.33 us
    pallas_call x1, Pallas kernels: 26.7 us -> 10.5 us  [attend_pages(): pl.pallas_call(functools.partial(pages_kernel, dim ** (-0.5)), out_shape=...]
    unnamed x14 -> x8, local copies, waits for them, and re-layouts: 3.81 us -> 1.33 us
    pallas_call x1, Pallas kernels: 27.1 us -> 25.6 us  [gather_queries(): pl.pallas_call(functools.partial(queries_kernel, pool.bit_length() - 1, p...]
where the time goes in v3:
time: 103 us
  Pallas kernels  101 us (98%)
  local copies, waits for them, and re-layouts  1.33 us (1%)
    pallas_call x1, Pallas kernels, finish(): pl.pallas_call(finish_kernel, out_shape=(jax.ShapeDtypeStruct((rows, 16,...  65 us
    pallas_call x1, Pallas kernels, gather_queries(): pl.pallas_call(functools.partial(queries_kernel, pool.bit_length() - 1, p...  25.6 us
    pallas_call x1, Pallas kernels, attend_pages(): pl.pallas_call(functools.partial(pages_kernel, dim ** (-0.5)), out_shape=...  10.5 us

profile of v3, /device:TPU:1, one launch (start us, length us, event | category | flops | bytes accessed | tf_op | source)
XLA Modules:
  0.0 103.2 jit_solution(5116077313221048082)
XLA Ops:
  0.6 0.0 copy-start
  0.6 0.0 copy-start.1
  0.7 25.6 %gather_queries.1 = (bf16[4,4,2,2,16,16,128]{6,5,4,3,2,1,0:T(8,128)(2,1)S(1)}, s32[24,128]{1,0:T(8,128)S(1)}) custom-call(bf16[2,16,16,128]{3,2,1,0:T(8,128)(2,1)} %bitcast.9, s32[32,1024]{1,0:T(8,128)} %bitcast.10, s32[8,128]{1,0:T(8,128)} %bitcast.11), custom_call_target="tpu_custom_call" | custom-call | flops 10000000000 | bytes 8388608 | tf_op jit(solution)/shard_map/gather_queries/pallas_call | solution.py:261
  26.3 0.0 copy-done
  26.3 0.0 copy-done.1
  26.3 0.0 copy-start.2
  26.3 10.5 %attend_pages.1.part_ref = f32[2,32,33,8,128]{4,3,2,1,0:T(8,128)S(1)} custom-call(s32[24,128]{1,0:T(8,128)S(1)} %get-tuple-element.4.list_ref, bf16[1024,16,128]{2,1,0:T(8,128)(2,1)S(1)} %bitcast.8, bf16[1024,32,128]{2,1,0:T(8,128)(2,1)S(1)} %bitcast.6, bf16[1024,32,128]{2,1,0:T(8,128)(2,1)S(1)} %bitcast.7), custom_call_target="tpu_custom_call" | custom-call | tf_op jit(solution)/shard_map/attend_pages/pallas_call | solution.py:361
  36.8 0.0 copy-done.2
  36.9 65.0 %finish.1 = (bf16[32,16,128]{2,1,0:T(8,128)(2,1)S(1)}, bf16[256,256]{1,0:T(8,128)(2,1)S(1)}) custom-call(f32[2,32,33,8,128]{4,3,2,1,0:T(8,128)S(1)} %attend_pages.1.part_ref, bf16[2048,256]{1,0:T(8,128)(2,1)S(1)} %copy-done.2), custom_call_target="tpu_custom_call" | custom-call | tf_op jit(solution)/shard_map/finish/pallas_call | solution.py:577
  101.9 0.7 copy.10
  102.6 0.7 copy.11
Async XLA Ops:
  0.6 25.7 %copy-start = (bf16[1024,16,2,128]{3,2,1,0:T(2,128)(2,1)S(1)}, bf16[1024,16,2,128]{3,2,1,0:T(2,128)(2,1)}, u32[]{:S(2)}) copy-start(bf16[1024,16,2,128]{3,2,1,0:T(2,128)(2,1)} %param.7) | copy-start | bytes 25165828
  0.6 25.7 %copy-start.1 = (bf16[1024,16,2,128]{3,2,1,0:T(2,128)(2,1)S(1)}, bf16[1024,16,2,128]{3,2,1,0:T(2,128)(2,1)}, u32[]{:S(2)}) copy-start(bf16[1024,16,2,128]{3,2,1,0:T(2,128)(2,1)} %param.8) | copy-start | bytes 25165828
  26.3 10.5 %copy-start.2 = (bf16[2048,256]{1,0:T(8,128)(2,1)S(1)}, bf16[2048,256]{1,0:T(8,128)(2,1)}, u32[]{:S(2)}) copy-start(bf16[2048,256]{1,0:T(8,128)(2,1)} %w_ref.1) | copy-start | bytes 3145732

commit v4 on v3

--- a/solution.py
+++ b/solution.py
@@ -11,6 +11,7 @@
 DP = ("dp_0", "dp_1", "dp_2")
 MESH = pl.DeviceIdType.MESH
 LOW = -1e30
+QUARTER = 64
 BATCH = 32
 NOTHING = 1056
 F32 = jnp.float32
@@ -52,13 +53,14 @@
     )
 
 
-def plane_gather(own, full, ssem, rsem, dsend, drecv, between=()):
+def plane_gather(own, full, ssem, rsem, dsend, drecv, between=(), row_done=None):
     z, y, c, s = place()
     work = list(between)
 
     def fill():
-        if work:
-            work.pop(0)()
+        piece = work.pop(0) if work else None
+        if piece is not None:
+            piece()
 
     def at(h, a, b):
         return full.at[a, b, c, h] if h == 0 else full.at[b, a, c, h]
@@ -120,10 +122,12 @@
         spread(h, 4, 12, at(h, far, b), far, b)
         share(h, 12, at(h, far, b), at(h, far, b))
     fill()
-    for group, step in ((1, 0), (2, -1), (3, 1), (4, 2)):
+    steps = (0, 0, -1, 1, 2)
+
+    def sides(group):
         for h in range(2):
             a, b = mine(h)
-            row = wrap(a + step * s)
+            row = wrap(a + steps[group] * s)
             near = wrap(b - s)
             come(h, group, 0, at(h, row, near))
             go(h, group, 2, at(h, row, near), at(h, row, near), device(h, a, wrap(b + s)))
@@ -132,17 +136,45 @@
             come(h, group, 1, at(h, row, other))
             share(h, 4 * (group - 1) + 2, at(h, row, other), at(h, row, other))
         fill()
-    for group, step in ((1, 0), (2, -1), (3, 1), (4, 2)):
+
+    def far(group):
         for h in range(2):
             a, b = mine(h)
-            row = wrap(a + step * s)
-            far = wrap(b + 2)
-            come(h, group, 2, at(h, row, far))
-            share(h, 4 * (group - 1) + 3, at(h, row, far), at(h, row, far))
-    for h in range(2):
-        for slot in range(16):
+            row = wrap(a + steps[group] * s)
+            opposite = wrap(b + 2)
+            come(h, group, 2, at(h, row, opposite))
+            share(h, 4 * (group - 1) + 3, at(h, row, opposite), at(h, row, opposite))
+
+    across = (0, 2, 1, 3)
+
+    def from_pair(k, n):
+        for h, slot in ((0, 4 * across[k] + across[n]), (1, 4 * across[n] + across[k])):
             where = full.at[0, 0, 1 - c, h]
             remote(where, where, dsend.at[h, slot], drecv.at[h, slot], plane_id(z, y, 1 - c)).wait_recv()
+
+    def arrived(k, columns=(0, 1, 2, 3)):
+        for n in columns:
+            from_pair(k, n)
+        if row_done is not None:
+            row_done(k, columns)
+
+    for group in range(1, 5):
+        sides(group)
+    far(1)
+    if row_done is not None:
+        arrived(0)
+    far(2)
+    far(3)
+    if row_done is not None:
+        arrived(1)
+        arrived(2)
+    far(4)
+    if row_done is not None:
+        arrived(3, (0, 1, 2))
+        arrived(3, (3,))
+    else:
+        for k in range(4):
+            arrived(k)
     return sent
 
 
@@ -218,18 +250,19 @@
         list_ref[16:24, :] = jnp.broadcast_to(number, (8, 128)).astype(jnp.int32)
         total_ref[...] = jnp.zeros_like(total_ref)
 
-    sub = lax.broadcasted_iota(jnp.int32, (128, 128), 0)
+    sub = lax.broadcasted_iota(jnp.int32, (128, 128), 0).astype(F32).astype(BF16)
+    one, nil = jnp.ones((128, 128), BF16), jnp.zeros((128, 128), BF16)
     sub8 = lax.broadcasted_iota(jnp.int32, (8, 128), 0)
 
     def scatter(part):
         def step(n, carry):
             base = pl.multiple_of(n * 8, 8)
-            lo8 = lo_ref[pl.ds(base, 8), :]
+            lo8 = lo_ref[pl.ds(base, 8), :].astype(F32)
             hi8 = hi_ref[pl.ds(base, 8), :]
             p8 = [part_ref[k, pl.ds(base, 8), :] for k in range(4)]
             wide, tall = [], []
             for r in range(8):
-                wide.append(jnp.where(sub == lo8[r:r + 1, :], 1.0, 0.0).astype(BF16))
+                wide.append(jnp.where(sub == jnp.broadcast_to(lo8[r:r + 1, :], (128, 128)).astype(BF16), one, nil))
                 hit = sub8 == hi8[r:r + 1, :]
                 tall.append(jnp.concatenate(
                     [jnp.where(hit, p8[k][r:r + 1, :], 0.0) for k in range(4)], axis=0).astype(BF16))
@@ -249,7 +282,15 @@
         tokens = (p2 >> 4) + 1
         list_ref[0:8, :] = page + (owner << 10) + (tokens << 20) + (p3 << 25)
 
-    pieces = [place_pages] + [functools.partial(scatter, n) for n in range(4)] + [write_list]
+    def start_list():
+        place_pages()
+        scatter(0)
+
+    def end_list():
+        scatter(3)
+        write_list()
+
+    pieces = [start_list, None, functools.partial(scatter, 1), None, functools.partial(scatter, 2), None, end_list]
     for copy in plane_gather(full_ref.at[z, y, c], full_ref, ssem, rsem, dsend, drecv, between=pieces):
         copy.wait_send()
 
@@ -417,15 +458,21 @@
         zt, yt = spot(hh, 0, sign * s)
         return plane_id(zt, yt, c)
 
-    order = (0, 2, 1, 3)
-
-    for oa in order:
-        def begin(k, carry, oa=oa):
-            hh, ob = k % 2, k // 2
-            zt, yt = spot(hh, step_of(oa), step_of(ob))
-            swap(hh, zt, yt).start()
+    def far_place(n):
+        m, odd = (n + 1) // 2, n % 2
+        return wrap(z + step_of((1 - odd) * m)), wrap(y + step_of(odd * m))
+
+    def rest_place(n):
+        m, k = n // 3, n % 3
+        return wrap(z + step_of(2 - m + 3 * (m // 2))), wrap(y + step_of(2 - k + 3 * (k // 2)))
+
+    def give(where):
+        def step(n, carry):
+            zt, yt = where(n)
+            for hh in range(2):
+                swap(hh, zt, yt).start()
             return carry
-        lax.fori_loop(0, 8, begin, 0)
+        return step
 
     def send1(kind, hh, ob, zt, yt):
         dst = (far1, near1, next1)[kind].at[hh, ob]
@@ -464,6 +511,8 @@
         both_cores(hh, zt, yt)
         return carry
 
+    lax.fori_loop(0, 7, give(far_place), 0)
+    lax.fori_loop(0, 9, give(rest_place), 0)
     lax.fori_loop(0, 8, far_units, 0)
     lax.fori_loop(0, 8, next_units, 0)
     lax.fori_loop(0, 8, near_units, 0)
@@ -521,34 +570,63 @@
     for hh in range(2):
         full[z, y, c, hh] = own[hh]
 
-    sent = plane_gather(own, full, ssem, rsem, dsend, drecv)
-
-    def project(step):
-        t = wrap(x + step)
-        rows = [full[t, :, :, hh, head].reshape(256, 128) for hh in range(2) for head in range(8)]
-        cols[t] = jnp.dot(jnp.concatenate(rows, axis=1), w_ref[...], preferred_element_type=F32)
-        return t
-
-    def sendx(kind, t):
-        return remote(cols.at[t], (farx, nearx, nextx)[kind], sx.at[kind], rx.at[kind],
+    def sendx(kind, t, q):
+        rows = pl.ds(pl.multiple_of(q * QUARTER, QUARTER) if not isinstance(q, int) else q * QUARTER, QUARTER)
+        dst = (farx, nearx, nextx)[kind].at[rows]
+        return remote(cols.at[t, rows], dst, sx.at[kind, q], rx.at[kind, q],
                       {"mp": wrap(x + (s if kind < 2 else -s))})
 
-    t = project(2)
-    sendx(0, t).start()
-    t = project(-s)
-    sendx(2, t).start()
-    t = project(s)
-    sendx(0, t).wait_recv()
-    cols[t] = cols[t] + farx[...]
-    sendx(1, t).start()
-    t = project(0)
-    sendx(2, t).wait_recv()
-    total = cols[t] + nextx[...]
-    sendx(1, t).wait_recv()
-    proj_ref[...] = (total + nearx[...]).astype(BF16)
+    targets = [wrap(z + step) for step in (0, -s, s, 2)]
+    columns_of = [wrap(y + step) for step in (0, -s, s, 2)]
+
+    def pass_on(k):
+        t = targets[k]
+
+        @pl.when(wrap(t - x - s) == 0)
+        def _():
+            for q in columns_of:
+                rows = pl.ds(pl.multiple_of(q * QUARTER, QUARTER), QUARTER)
+                sendx(0, t, q).wait_recv()
+                cols[t, rows] = cols[t, rows] + farx[rows]
+                sendx(1, t, q).start()
+
+    def send_on(t, quarters):
+        @pl.when(wrap(t - x - 2) == 0)
+        def _():
+            for q in quarters:
+                sendx(0, t, q).start()
+
+        @pl.when(wrap(t - x + s) == 0)
+        def _():
+            for q in quarters:
+                sendx(2, t, q).start()
+
+    def project(k, columns):
+        t = targets[k]
+        if len(columns) == 4:
+            rows = [full[t, :, :, hh, head].reshape(256, 128) for hh in range(2) for head in range(8)]
+            cols[t] = jnp.dot(jnp.concatenate(rows, axis=1), w_ref[...], preferred_element_type=F32)
+            send_on(t, columns_of)
+            return
+        for n in columns:
+            q = columns_of[n]
+            rows = [full[t, q, :, hh, head].reshape(QUARTER, 128) for hh in range(2) for head in range(8)]
+            cols[t, pl.ds(pl.multiple_of(q * QUARTER, QUARTER), QUARTER)] = jnp.dot(
+                jnp.concatenate(rows, axis=1), w_ref[...], preferred_element_type=F32)
+            send_on(t, [q])
+
+    sent = plane_gather(own, full, ssem, rsem, dsend, drecv, row_done=project)
+    for k in range(4):
+        pass_on(k)
+    for q in range(4):
+        rows = pl.ds(q * QUARTER, QUARTER)
+        sendx(2, x, q).wait_recv()
+        sendx(1, x, q).wait_recv()
+        proj_ref[rows] = (cols[x, rows] + nextx[rows] + nearx[rows]).astype(BF16)
 
     for kind in range(3):
-        sendx(kind, t).wait_send()
+        for q in range(4):
+            sendx(kind, x, q).wait_send()
     for copy in sent:
         copy.wait_send()
 
@@ -604,7 +682,7 @@
             dma((3, 2, 4)),
             dma((3, 2)),
             dma((3, 2)),
-        ] + gather_sems() + [dma((3,)), dma((3,))],
+        ] + gather_sems() + [dma((3, 4)), dma((3, 4))],
         compiler_params=pltpu.CompilerParams(collective_id=1, has_side_effects=True, vmem_limit_bytes=24 << 20),
         name="finish",
     )(parts, weight)

time: 103 us -> 98.9 us (0.960)
  Pallas kernels: 101 us -> 96.2 us
    pallas_call x1, Pallas kernels: 65 us -> 59.7 us  [finish(): pl.pallas_call(finish_kernel, out_shape=(jax.ShapeDtypeStruct((rows, 16,...]
where the time goes in v4:
time: 98.9 us; the launch traced here: 98.2 us
  Pallas kernels  96.2 us (97%)
  local copies, waits for them, and re-layouts  1.33 us (1%)
    pallas_call x1, Pallas kernels, finish(): pl.pallas_call(finish_kernel, out_shape=(jax.ShapeDtypeStruct((rows, 16,...  59.7 us
    pallas_call x1, Pallas kernels, gather_queries(): pl.pallas_call(functools.partial(queries_kernel, pool.bit_length() - 1, p...  25.4 us
    pallas_call x1, Pallas kernels, attend_pages(): pl.pallas_call(functools.partial(pages_kernel, dim ** (-0.5)), out_shape=...  11.1 us

profile of v4, /device:TPU:1, one launch (start us, length us, event | category | flops | bytes accessed | tf_op | source)
XLA Modules:
  0.0 98.2 jit_solution(2354897423457640198)
XLA Ops:
  0.6 0.0 copy-start
  0.6 0.0 copy-start.1
  0.7 25.4 %gather_queries.1 = (bf16[4,4,2,2,16,16,128]{6,5,4,3,2,1,0:T(8,128)(2,1)S(1)}, s32[24,128]{1,0:T(8,128)S(1)}) custom-call(bf16[2,16,16,128]{3,2,1,0:T(8,128)(2,1)} %bitcast.9, s32[32,1024]{1,0:T(8,128)} %bitcast.10, s32[8,128]{1,0:T(8,128)} %bitcast.11), custom_call_target="tpu_custom_call" | custom-call | flops 10000000000 | bytes 8388608 | tf_op jit(solution)/shard_map/gather_queries/pallas_call | solution.py:302
  26.1 0.0 copy-done
  26.1 0.0 copy-done.1
  26.1 0.0 copy-start.2
  26.1 11.1 %attend_pages.1.part_ref = f32[2,32,33,8,128]{4,3,2,1,0:T(8,128)S(1)} custom-call(s32[24,128]{1,0:T(8,128)S(1)} %get-tuple-element.4.list_ref, bf16[1024,16,128]{2,1,0:T(8,128)(2,1)S(1)} %bitcast.8, bf16[1024,32,128]{2,1,0:T(8,128)(2,1)S(1)} %bitcast.6, bf16[1024,32,128]{2,1,0:T(8,128)(2,1)S(1)} %bitcast.7), custom_call_target="tpu_custom_call" | custom-call | tf_op jit(solution)/shard_map/attend_pages/pallas_call | solution.py:402
  37.2 0.0 copy-done.2
  37.2 59.7 %finish.1 = (bf16[32,16,128]{2,1,0:T(8,128)(2,1)S(1)}, bf16[256,256]{1,0:T(8,128)(2,1)S(1)}) custom-call(f32[2,32,33,8,128]{4,3,2,1,0:T(8,128)S(1)} %attend_pages.1.part_ref, bf16[2048,256]{1,0:T(8,128)(2,1)S(1)} %copy-done.2), custom_call_target="tpu_custom_call" | custom-call | tf_op jit(solution)/shard_map/finish/pallas_call | solution.py:655
  96.9 0.7 copy.10
  97.5 0.7 copy.11
Async XLA Ops:
  0.6 25.4 %copy-start = (bf16[1024,16,2,128]{3,2,1,0:T(2,128)(2,1)S(1)}, bf16[1024,16,2,128]{3,2,1,0:T(2,128)(2,1)}, u32[]{:S(2)}) copy-start(bf16[1024,16,2,128]{3,2,1,0:T(2,128)(2,1)} %param.7) | copy-start | bytes 25165828
  0.6 25.4 %copy-start.1 = (bf16[1024,16,2,128]{3,2,1,0:T(2,128)(2,1)S(1)}, bf16[1024,16,2,128]{3,2,1,0:T(2,128)(2,1)}, u32[]{:S(2)}) copy-start(bf16[1024,16,2,128]{3,2,1,0:T(2,128)(2,1)} %param.8) | copy-start | bytes 25165828
  26.1 11.1 %copy-start.2 = (bf16[2048,256]{1,0:T(8,128)(2,1)S(1)}, bf16[2048,256]{1,0:T(8,128)(2,1)}, u32[]{:S(2)}) copy-start(bf16[2048,256]{1,0:T(8,128)(2,1)} %w_ref.1) | copy-start | bytes 3145732

commit v5 on v4

--- a/solution.py
+++ b/solution.py
@@ -124,18 +124,23 @@
     fill()
     steps = (0, 0, -1, 1, 2)
 
-    def sides(group):
+    def near(group):
         for h in range(2):
             a, b = mine(h)
             row = wrap(a + steps[group] * s)
-            near = wrap(b - s)
-            come(h, group, 0, at(h, row, near))
-            go(h, group, 2, at(h, row, near), at(h, row, near), device(h, a, wrap(b + s)))
-            share(h, 4 * (group - 1) + 1, at(h, row, near), at(h, row, near))
-            other = wrap(b + s)
-            come(h, group, 1, at(h, row, other))
-            share(h, 4 * (group - 1) + 2, at(h, row, other), at(h, row, other))
+            side = wrap(b - s)
+            come(h, group, 0, at(h, row, side))
+            go(h, group, 2, at(h, row, side), at(h, row, side), device(h, a, wrap(b + s)))
+            share(h, 4 * (group - 1) + 1, at(h, row, side), at(h, row, side))
         fill()
+
+    def other(group):
+        for h in range(2):
+            a, b = mine(h)
+            row = wrap(a + steps[group] * s)
+            side = wrap(b + s)
+            come(h, group, 1, at(h, row, side))
+            share(h, 4 * (group - 1) + 2, at(h, row, side), at(h, row, side))
 
     def far(group):
         for h in range(2):
@@ -158,8 +163,14 @@
         if row_done is not None:
             row_done(k, columns)
 
-    for group in range(1, 5):
-        sides(group)
+    near(1)
+    near(2)
+    other(1)
+    near(3)
+    other(2)
+    near(4)
+    other(3)
+    other(4)
     far(1)
     if row_done is not None:
         arrived(0)
@@ -337,15 +348,15 @@
     token = (lane % 32) // 2
     token_of = [jnp.where(kv_match & (lane // 32 == n), token, 1 << 20) for n in range(4)]
 
-    def entry(k):
-        word = list_ref[k >> 7, k & 127]
+    def entry(base, e):
+        word = list_ref[base // 128, base % 128 + e]
         return word & 1023, (word >> 10) & 1023, (word >> 20) & 31, (word >> 25) & 1
 
     def step(n, carry):
         past = jnp.maximum(n - 1, 0) * BATCH
         base = n * BATCH
-        before = [entry(past + e) for e in range(BATCH)]
-        now = [entry(base + e) for e in range(BATCH)]
+        before = [entry(past, e) for e in range(BATCH)]
+        now = [entry(base, e) for e in range(BATCH)]
         outs, scores = [], []
         for g in range(BATCH // 4):
             four = slice(4 * g, 4 * g + 4)
@@ -383,9 +394,9 @@
 
     def spread(d, carry):
         tops = blank
+        line, first = 8 + d // 4, (d % 4) * 32
         for row in range(32):
-            r = d * 32 + row
-            last = list_ref[8 + (r >> 7), r & 127]
+            last = list_ref[line, first + row]
             acc = sum_ref[last]
             tops = jnp.where((lane == row) | (lane == row + 32), top_ref[last], tops)
             for hh in range(2):

time: 98.9 us -> 97.4 us (0.985)
  Pallas kernels: 96.2 us -> 94.3 us
    pallas_call x1, Pallas kernels: 25.4 us -> 23.5 us  [gather_queries(): pl.pallas_call(functools.partial(queries_kernel, pool.bit_length() - 1, p...]
where the time goes in v5:
time: 97.4 us; the launch traced here: 96.3 us
  Pallas kernels  94.3 us (97%)
  local copies, waits for them, and re-layouts  1.33 us (1%)
    pallas_call x1, Pallas kernels, finish(): pl.pallas_call(finish_kernel, out_shape=(jax.ShapeDtypeStruct((rows, 16,...  60 us
    pallas_call x1, Pallas kernels, gather_queries(): pl.pallas_call(functools.partial(queries_kernel, pool.bit_length() - 1, p...  23.5 us
    pallas_call x1, Pallas kernels, attend_pages(): pl.pallas_call(functools.partial(pages_kernel, dim ** (-0.5)), out_shape=...  10.8 us

profile of v5, /device:TPU:1, one launch (start us, length us, event | category | flops | bytes accessed | tf_op | source)
XLA Modules:
  0.0 96.3 jit_solution(1134817304837486219)
XLA Ops:
  0.6 0.0 copy-start
  0.6 0.0 copy-start.1
  0.7 23.5 %gather_queries.1 = (bf16[4,4,2,2,16,16,128]{6,5,4,3,2,1,0:T(8,128)(2,1)S(1)}, s32[24,128]{1,0:T(8,128)S(1)}) custom-call(bf16[2,16,16,128]{3,2,1,0:T(8,128)(2,1)} %bitcast.9, s32[32,1024]{1,0:T(8,128)} %bitcast.10, s32[8,128]{1,0:T(8,128)} %bitcast.11), custom_call_target="tpu_custom_call" | custom-call | flops 10000000000 | bytes 8388608 | tf_op jit(solution)/shard_map/gather_queries/pallas_call | solution.py:313
  24.2 0.0 copy-done
  24.2 0.0 copy-done.1
  24.2 0.0 copy-start.2
  24.2 10.8 %attend_pages.1.part_ref = f32[2,32,33,8,128]{4,3,2,1,0:T(8,128)S(1)} custom-call(s32[24,128]{1,0:T(8,128)S(1)} %get-tuple-element.4.list_ref, bf16[1024,16,128]{2,1,0:T(8,128)(2,1)S(1)} %bitcast.8, bf16[1024,32,128]{2,1,0:T(8,128)(2,1)S(1)} %bitcast.6, bf16[1024,32,128]{2,1,0:T(8,128)(2,1)S(1)} %bitcast.7), custom_call_target="tpu_custom_call" | custom-call | tf_op jit(solution)/shard_map/attend_pages/pallas_call | solution.py:413
  35.0 0.0 copy-done.2
  35.0 60.0 %finish.1 = (bf16[32,16,128]{2,1,0:T(8,128)(2,1)S(1)}, bf16[256,256]{1,0:T(8,128)(2,1)S(1)}) custom-call(f32[2,32,33,8,128]{4,3,2,1,0:T(8,128)S(1)} %attend_pages.1.part_ref, bf16[2048,256]{1,0:T(8,128)(2,1)S(1)} %copy-done.2), custom_call_target="tpu_custom_call" | custom-call | tf_op jit(solution)/shard_map/finish/pallas_call | solution.py:666
  95.0 0.7 copy.10
  95.7 0.7 copy.11
Async XLA Ops:
  0.6 23.5 %copy-start = (bf16[1024,16,2,128]{3,2,1,0:T(2,128)(2,1)S(1)}, bf16[1024,16,2,128]{3,2,1,0:T(2,128)(2,1)}, u32[]{:S(2)}) copy-start(bf16[1024,16,2,128]{3,2,1,0:T(2,128)(2,1)} %param.7) | copy-start | bytes 25165828
  0.6 23.5 %copy-start.1 = (bf16[1024,16,2,128]{3,2,1,0:T(2,128)(2,1)S(1)}, bf16[1024,16,2,128]{3,2,1,0:T(2,128)(2,1)}, u32[]{:S(2)}) copy-start(bf16[1024,16,2,128]{3,2,1,0:T(2,128)(2,1)} %param.8) | copy-start | bytes 25165828
  24.2 10.8 %copy-start.2 = (bf16[2048,256]{1,0:T(8,128)(2,1)S(1)}, bf16[2048,256]{1,0:T(8,128)(2,1)}, u32[]{:S(2)}) copy-start(bf16[2048,256]{1,0:T(8,128)(2,1)} %w_ref.1) | copy-start | bytes 3145732

commit v6 on v5

--- a/solution.py
+++ b/solution.py
@@ -296,12 +296,9 @@
     def start_list():
         place_pages()
         scatter(0)
-
-    def end_list():
-        scatter(3)
-        write_list()
-
-    pieces = [start_list, None, functools.partial(scatter, 1), None, functools.partial(scatter, 2), None, end_list]
+        scatter(1)
+
+    pieces = [start_list, None, functools.partial(scatter, 2), functools.partial(scatter, 3), None, None, write_list]
     for copy in plane_gather(full_ref.at[z, y, c], full_ref, ssem, rsem, dsend, drecv, between=pieces):
         copy.wait_send()
 
@@ -551,8 +548,12 @@
         send2(2, hh, zt, yt).start()
         return carry
 
+    def near_sums(hh, carry):
+        gathered(hh, 1)
+        return carry
+
     def near_blocks(hh, carry):
-        zt, yt = gathered(hh, 1)
+        zt, yt = spot(hh, 0, s)
         send2(0, hh, zt, yt).wait_recv()
         merge(unit.at[hh, zt, yt], unit.at[hh, zt, yt], far2.at[hh])
         send2(1, hh, zt, yt).start()
@@ -566,7 +567,7 @@
         merge(unit.at[hh, zt, yt], unit.at[hh, zt, yt], near2.at[hh])
         return carry
 
-    for phase in (far_blocks, next_blocks, near_blocks, own_blocks):
+    for phase in (far_blocks, near_sums, next_blocks, near_blocks, own_blocks):
         lax.fori_loop(0, 2, phase, 0)
 
     masses = [unit[hh, z, y, 32] for hh in range(2)]
@@ -629,8 +630,8 @@
     sent = plane_gather(own, full, ssem, rsem, dsend, drecv, row_done=project)
     for k in range(4):
         pass_on(k)
-    for q in range(4):
-        rows = pl.ds(q * QUARTER, QUARTER)
+    for q in columns_of:
+        rows = pl.ds(pl.multiple_of(q * QUARTER, QUARTER), QUARTER)
         sendx(2, x, q).wait_recv()
         sendx(1, x, q).wait_recv()
         proj_ref[rows] = (cols[x, rows] + nextx[rows] + nearx[rows]).astype(BF16)

time: 97.4 us -> 96.4 us (0.990); the launches traced: 96.3 us -> 96.4 us
  no operation moved by 1% of the time
where the time goes in v6:
time: 96.4 us
  Pallas kernels  94.4 us (98%)
  local copies, waits for them, and re-layouts  1.33 us (1%)
    pallas_call x1, Pallas kernels, finish(): pl.pallas_call(finish_kernel, out_shape=(jax.ShapeDtypeStruct((rows, 16,...  60.9 us
    pallas_call x1, Pallas kernels, gather_queries(): pl.pallas_call(functools.partial(queries_kernel, pool.bit_length() - 1, p...  23.2 us
    pallas_call x1, Pallas kernels, attend_pages(): pl.pallas_call(functools.partial(pages_kernel, dim ** (-0.5)), out_shape=...  10.2 us

profile of v6, /device:TPU:1, one launch (start us, length us, event | category | flops | bytes accessed | tf_op | source)
XLA Modules:
  0.0 96.4 jit_solution(6079160822623528313)
XLA Ops:
  0.6 0.0 copy-start
  0.6 0.0 copy-start.1
  0.7 23.2 %gather_queries.1 = (bf16[4,4,2,2,16,16,128]{6,5,4,3,2,1,0:T(8,128)(2,1)S(1)}, s32[24,128]{1,0:T(8,128)S(1)}) custom-call(bf16[2,16,16,128]{3,2,1,0:T(8,128)(2,1)} %bitcast.9, s32[32,1024]{1,0:T(8,128)} %bitcast.10, s32[8,128]{1,0:T(8,128)} %bitcast.11), custom_call_target="tpu_custom_call" | custom-call | flops 10000000000 | bytes 8388608 | tf_op jit(solution)/shard_map/gather_queries/pallas_call | solution.py:310
  23.9 0.0 copy-done
  23.9 0.0 copy-done.1
  23.9 0.0 copy-start.2
  23.9 10.2 %attend_pages.1.part_ref = f32[2,32,33,8,128]{4,3,2,1,0:T(8,128)S(1)} custom-call(s32[24,128]{1,0:T(8,128)S(1)} %get-tuple-element.4.list_ref, bf16[1024,16,128]{2,1,0:T(8,128)(2,1)S(1)} %bitcast.8, bf16[1024,32,128]{2,1,0:T(8,128)(2,1)S(1)} %bitcast.6, bf16[1024,32,128]{2,1,0:T(8,128)(2,1)S(1)} %bitcast.7), custom_call_target="tpu_custom_call" | custom-call | tf_op jit(solution)/shard_map/attend_pages/pallas_call | solution.py:410
  34.1 0.0 copy-done.2
  34.2 60.9 %finish.1 = (bf16[32,16,128]{2,1,0:T(8,128)(2,1)S(1)}, bf16[256,256]{1,0:T(8,128)(2,1)S(1)}) custom-call(f32[2,32,33,8,128]{4,3,2,1,0:T(8,128)S(1)} %attend_pages.1.part_ref, bf16[2048,256]{1,0:T(8,128)(2,1)S(1)} %copy-done.2), custom_call_target="tpu_custom_call" | custom-call | tf_op jit(solution)/shard_map/finish/pallas_call | solution.py:667
  95.1 0.7 copy.10
  95.8 0.7 copy.11
Async XLA Ops:
  0.6 23.3 %copy-start = (bf16[1024,16,2,128]{3,2,1,0:T(2,128)(2,1)S(1)}, bf16[1024,16,2,128]{3,2,1,0:T(2,128)(2,1)}, u32[]{:S(2)}) copy-start(bf16[1024,16,2,128]{3,2,1,0:T(2,128)(2,1)} %param.7) | copy-start | bytes 25165828
  0.6 23.3 %copy-start.1 = (bf16[1024,16,2,128]{3,2,1,0:T(2,128)(2,1)S(1)}, bf16[1024,16,2,128]{3,2,1,0:T(2,128)(2,1)}, u32[]{:S(2)}) copy-start(bf16[1024,16,2,128]{3,2,1,0:T(2,128)(2,1)} %param.8) | copy-start | bytes 25165828
  23.9 10.2 %copy-start.2 = (bf16[2048,256]{1,0:T(8,128)(2,1)S(1)}, bf16[2048,256]{1,0:T(8,128)(2,1)}, u32[]{:S(2)}) copy-start(bf16[2048,256]{1,0:T(8,128)(2,1)} %w_ref.1) | copy-start | bytes 3145732

commit v7 on v6

--- a/solution.py
+++ b/solution.py
@@ -528,7 +528,7 @@
 
     def send2(kind, hh, zt, yt):
         dst = (far2, near2, next2)[kind].at[hh]
-        return remote(unit.at[hh, zt, yt], dst, s2.at[kind, hh], r2.at[kind, hh], hop2(hh, 1 if kind < 2 else -1))
+        return remote(unit.at[hh, zt, yt], dst, s2.at[kind, hh], r2.at[kind, hh], hop2(hh, -1 if kind < 2 else 1))
 
     def gathered(hh, ob):
         zt, yt = spot(hh, 0, step_of(ob))
@@ -544,16 +544,16 @@
         return carry
 
     def next_blocks(hh, carry):
-        zt, yt = gathered(hh, 2)
+        zt, yt = gathered(hh, 1)
         send2(2, hh, zt, yt).start()
         return carry
 
     def near_sums(hh, carry):
-        gathered(hh, 1)
+        gathered(hh, 2)
         return carry
 
     def near_blocks(hh, carry):
-        zt, yt = spot(hh, 0, s)
+        zt, yt = spot(hh, 0, -s)
         send2(0, hh, zt, yt).wait_recv()
         merge(unit.at[hh, zt, yt], unit.at[hh, zt, yt], far2.at[hh])
         send2(1, hh, zt, yt).start()
@@ -567,7 +567,7 @@
         merge(unit.at[hh, zt, yt], unit.at[hh, zt, yt], near2.at[hh])
         return carry
 
-    for phase in (far_blocks, near_sums, next_blocks, near_blocks, own_blocks):
+    for phase in (far_blocks, next_blocks, near_sums, near_blocks, own_blocks):
         lax.fori_loop(0, 2, phase, 0)
 
     masses = [unit[hh, z, y, 32] for hh in range(2)]

time: 96.4 us -> 94.9 us (0.984)
  Pallas kernels: 94.4 us -> 92.7 us
    pallas_call x1, Pallas kernels: 60.9 us -> 59.2 us  [finish(): pl.pallas_call(finish_kernel, out_shape=(jax.ShapeDtypeStruct((rows, 16,...]
where the time goes in v7:
time: 94.9 us; the launch traced here: 94.7 us
  Pallas kernels  92.7 us (98%)
  local copies, waits for them, and re-layouts  1.33 us (1%)
    pallas_call x1, Pallas kernels, finish(): pl.pallas_call(finish_kernel, out_shape=(jax.ShapeDtypeStruct((rows, 16,...  59.2 us
    pallas_call x1, Pallas kernels, gather_queries(): pl.pallas_call(functools.partial(queries_kernel, pool.bit_length() - 1, p...  23.2 us
    pallas_call x1, Pallas kernels, attend_pages(): pl.pallas_call(functools.partial(pages_kernel, dim ** (-0.5)), out_shape=...  10.2 us

profile of v7, /device:TPU:1, one launch (start us, length us, event | category | flops | bytes accessed | tf_op | source)
XLA Modules:
  0.0 94.7 jit_solution(13384636030679913734)
XLA Ops:
  0.6 0.0 copy-start
  0.6 0.0 copy-start.1
  0.7 23.2 %gather_queries.1 = (bf16[4,4,2,2,16,16,128]{6,5,4,3,2,1,0:T(8,128)(2,1)S(1)}, s32[24,128]{1,0:T(8,128)S(1)}) custom-call(bf16[2,16,16,128]{3,2,1,0:T(8,128)(2,1)} %bitcast.9, s32[32,1024]{1,0:T(8,128)} %bitcast.10, s32[8,128]{1,0:T(8,128)} %bitcast.11), custom_call_target="tpu_custom_call" | custom-call | flops 10000000000 | bytes 8388608 | tf_op jit(solution)/shard_map/gather_queries/pallas_call | solution.py:310
  23.9 0.0 copy-done
  23.9 0.0 copy-done.1
  23.9 0.0 copy-start.2
  23.9 10.2 %attend_pages.1.part_ref = f32[2,32,33,8,128]{4,3,2,1,0:T(8,128)S(1)} custom-call(s32[24,128]{1,0:T(8,128)S(1)} %get-tuple-element.4.list_ref, bf16[1024,16,128]{2,1,0:T(8,128)(2,1)S(1)} %bitcast.8, bf16[1024,32,128]{2,1,0:T(8,128)(2,1)S(1)} %bitcast.6, bf16[1024,32,128]{2,1,0:T(8,128)(2,1)S(1)} %bitcast.7), custom_call_target="tpu_custom_call" | custom-call | tf_op jit(solution)/shard_map/attend_pages/pallas_call | solution.py:410
  34.2 0.0 copy-done.2
  34.2 59.2 %finish.1 = (bf16[32,16,128]{2,1,0:T(8,128)(2,1)S(1)}, bf16[256,256]{1,0:T(8,128)(2,1)S(1)}) custom-call(f32[2,32,33,8,128]{4,3,2,1,0:T(8,128)S(1)} %attend_pages.1.part_ref, bf16[2048,256]{1,0:T(8,128)(2,1)S(1)} %copy-done.2), custom_call_target="tpu_custom_call" | custom-call | tf_op jit(solution)/shard_map/finish/pallas_call | solution.py:667
  93.4 0.7 copy.10
  94.0 0.7 copy.11
Async XLA Ops:
  0.6 23.3 %copy-start = (bf16[1024,16,2,128]{3,2,1,0:T(2,128)(2,1)S(1)}, bf16[1024,16,2,128]{3,2,1,0:T(2,128)(2,1)}, u32[]{:S(2)}) copy-start(bf16[1024,16,2,128]{3,2,1,0:T(2,128)(2,1)} %param.7) | copy-start | bytes 25165828
  0.6 23.3 %copy-start.1 = (bf16[1024,16,2,128]{3,2,1,0:T(2,128)(2,1)S(1)}, bf16[1024,16,2,128]{3,2,1,0:T(2,128)(2,1)}, u32[]{:S(2)}) copy-start(bf16[1024,16,2,128]{3,2,1,0:T(2,128)(2,1)} %param.8) | copy-start | bytes 25165828
  23.9 10.3 %copy-start.2 = (bf16[2048,256]{1,0:T(8,128)(2,1)S(1)}, bf16[2048,256]{1,0:T(8,128)(2,1)}, u32[]{:S(2)}) copy-start(bf16[2048,256]{1,0:T(8,128)(2,1)} %w_ref.1) | copy-start | bytes 3145732

commit v8 on v7

--- a/solution.py
+++ b/solution.py
@@ -520,8 +520,9 @@
         return carry
 
     lax.fori_loop(0, 7, give(far_place), 0)
+    lax.fori_loop(0, 2, far_units, 0)
     lax.fori_loop(0, 9, give(rest_place), 0)
-    lax.fori_loop(0, 8, far_units, 0)
+    lax.fori_loop(2, 8, far_units, 0)
     lax.fori_loop(0, 8, next_units, 0)
     lax.fori_loop(0, 8, near_units, 0)
     lax.fori_loop(0, 8, own_units, 0)

time: 94.9 us -> 94.9 us (level)
  no operation moved by 1% of the time
where the time goes in v8:
time: 94.9 us; the launch traced here: 94.7 us
  Pallas kernels  92.6 us (98%)
  local copies, waits for them, and re-layouts  1.33 us (1%)
    pallas_call x1, Pallas kernels, finish(): pl.pallas_call(finish_kernel, out_shape=(jax.ShapeDtypeStruct((rows, 16,...  59.2 us
    pallas_call x1, Pallas kernels, gather_queries(): pl.pallas_call(functools.partial(queries_kernel, pool.bit_length() - 1, p...  23.2 us
    pallas_call x1, Pallas kernels, attend_pages(): pl.pallas_call(functools.partial(pages_kernel, dim ** (-0.5)), out_shape=...  10.2 us

profile of v8, /device:TPU:1, one launch (start us, length us, event | category | flops | bytes accessed | tf_op | source)
XLA Modules:
  0.0 94.7 jit_solution(9419306412230137673)
XLA Ops:
  0.6 0.0 copy-start
  0.6 0.0 copy-start.1
  0.7 23.2 %gather_queries.1 = (bf16[4,4,2,2,16,16,128]{6,5,4,3,2,1,0:T(8,128)(2,1)S(1)}, s32[24,128]{1,0:T(8,128)S(1)}) custom-call(bf16[2,16,16,128]{3,2,1,0:T(8,128)(2,1)} %bitcast.9, s32[32,1024]{1,0:T(8,128)} %bitcast.10, s32[8,128]{1,0:T(8,128)} %bitcast.11), custom_call_target="tpu_custom_call" | custom-call | flops 10000000000 | bytes 8388608 | tf_op jit(solution)/shard_map/gather_queries/pallas_call | solution.py:310
  23.9 0.0 copy-done
  23.9 0.0 copy-done.1
  23.9 0.0 copy-start.2
  23.9 10.2 %attend_pages.1.part_ref = f32[2,32,33,8,128]{4,3,2,1,0:T(8,128)S(1)} custom-call(s32[24,128]{1,0:T(8,128)S(1)} %get-tuple-element.4.list_ref, bf16[1024,16,128]{2,1,0:T(8,128)(2,1)S(1)} %bitcast.8, bf16[1024,32,128]{2,1,0:T(8,128)(2,1)S(1)} %bitcast.6, bf16[1024,32,128]{2,1,0:T(8,128)(2,1)S(1)} %bitcast.7), custom_call_target="tpu_custom_call" | custom-call | tf_op jit(solution)/shard_map/attend_pages/pallas_call | solution.py:410
  34.1 0.0 copy-done.2
  34.2 59.2 %finish.1 = (bf16[32,16,128]{2,1,0:T(8,128)(2,1)S(1)}, bf16[256,256]{1,0:T(8,128)(2,1)S(1)}) custom-call(f32[2,32,33,8,128]{4,3,2,1,0:T(8,128)S(1)} %attend_pages.1.part_ref, bf16[2048,256]{1,0:T(8,128)(2,1)S(1)} %copy-done.2), custom_call_target="tpu_custom_call" | custom-call | tf_op jit(solution)/shard_map/finish/pallas_call | solution.py:668
  93.4 0.7 copy.10
  94.0 0.7 copy.11
Async XLA Ops:
  0.6 23.3 %copy-start = (bf16[1024,16,2,128]{3,2,1,0:T(2,128)(2,1)S(1)}, bf16[1024,16,2,128]{3,2,1,0:T(2,128)(2,1)}, u32[]{:S(2)}) copy-start(bf16[1024,16,2,128]{3,2,1,0:T(2,128)(2,1)} %param.7) | copy-start | bytes 25165828
  0.6 23.3 %copy-start.1 = (bf16[1024,16,2,128]{3,2,1,0:T(2,128)(2,1)S(1)}, bf16[1024,16,2,128]{3,2,1,0:T(2,128)(2,1)}, u32[]{:S(2)}) copy-start(bf16[1024,16,2,128]{3,2,1,0:T(2,128)(2,1)} %param.8) | copy-start | bytes 25165828
  23.9 10.2 %copy-start.2 = (bf16[2048,256]{1,0:T(8,128)(2,1)S(1)}, bf16[2048,256]{1,0:T(8,128)(2,1)}, u32[]{:S(2)}) copy-start(bf16[2048,256]{1,0:T(8,128)(2,1)} %w_ref.1) | copy-start | bytes 3145732

commit v9 on v7

--- a/solution.py
+++ b/solution.py
@@ -705,8 +705,9 @@
     pool, page_len, kv, dim = lookup_sheets.shape
     rows, heads, _ = queries.shape
     all_queries, words = gather_queries(
+        queries.reshape(2, rows // 2, heads, dim),
         *(pltpu.with_memory_space_constraint(a, pltpu.HBM)
-          for a in (queries.reshape(2, rows // 2, heads, dim), page_table.T, context_len.reshape(req // 128, 128))),
+          for a in (page_table.T, context_len.reshape(req // 128, 128))),
         pool,
         page_len,
     )

time: 94.9 us -> 95.4 us (level)
    unnamed x8 -> x10, local copies, waits for them, and re-layouts: 1.33 us -> 2.22 us
where the time goes in v9:
time: 95.4 us; the launch traced here: 95.2 us
  Pallas kernels  92.3 us (97%)
  local copies, waits for them, and re-layouts  2.22 us (2%)
    pallas_call x1, Pallas kernels, finish(): pl.pallas_call(finish_kernel, out_shape=(jax.ShapeDtypeStruct((rows, 16,...  58.8 us
    pallas_call x1, Pallas kernels, gather_queries(): pl.pallas_call(functools.partial(queries_kernel, pool.bit_length() - 1, p...  23.3 us
    pallas_call x1, Pallas kernels, attend_pages(): pl.pallas_call(functools.partial(pages_kernel, dim ** (-0.5)), out_shape=...  10.2 us
    unnamed x10, local copies, waits for them, and re-layouts  2.22 us

profile of v9, /device:TPU:1, one launch (start us, length us, event | category | flops | bytes accessed | tf_op | source)
XLA Modules:
  0.0 95.2 jit_solution(11489489362506010531)
XLA Ops:
  0.6 0.0 copy-start.3
  0.6 0.9 copy-done.3
  1.5 0.0 copy-start
  1.5 0.0 copy-start.1
  1.5 23.3 %gather_queries.1 = (bf16[4,4,2,2,16,16,128]{6,5,4,3,2,1,0:T(8,128)(2,1)S(1)}, s32[24,128]{1,0:T(8,128)S(1)}) custom-call(bf16[2,16,16,128]{3,2,1,0:T(8,128)(2,1)S(1)} %bitcast.9, s32[32,1024]{1,0:T(8,128)} %bitcast.10, s32[8,128]{1,0:T(8,128)} %bitcast.11), custom_call_target="tpu_custom_call" | custom-call | flops 10000000000 | bytes 8388608 | tf_op jit(solution)/shard_map/gather_queries/pallas_call | solution.py:310
  24.8 0.0 copy-done
  24.8 0.0 copy-done.1
  24.9 0.0 copy-start.2
  24.9 10.2 %attend_pages.1.part_ref = f32[2,32,33,8,128]{4,3,2,1,0:T(8,128)S(1)} custom-call(s32[24,128]{1,0:T(8,128)S(1)} %get-tuple-element.4.list_ref, bf16[1024,16,128]{2,1,0:T(8,128)(2,1)S(1)} %bitcast.8, bf16[1024,32,128]{2,1,0:T(8,128)(2,1)S(1)} %bitcast.6, bf16[1024,32,128]{2,1,0:T(8,128)(2,1)S(1)} %bitcast.7), custom_call_target="tpu_custom_call" | custom-call | tf_op jit(solution)/shard_map/attend_pages/pallas_call | solution.py:410
  35.1 0.0 copy-done.2
  35.1 58.8 %finish.1 = (bf16[32,16,128]{2,1,0:T(8,128)(2,1)S(1)}, bf16[256,256]{1,0:T(8,128)(2,1)S(1)}) custom-call(f32[2,32,33,8,128]{4,3,2,1,0:T(8,128)S(1)} %attend_pages.1.part_ref, bf16[2048,256]{1,0:T(8,128)(2,1)S(1)} %copy-done.2), custom_call_target="tpu_custom_call" | custom-call | tf_op jit(solution)/shard_map/finish/pallas_call | solution.py:667
  93.9 0.7 copy.10
  94.5 0.7 copy.11
Async XLA Ops:
  0.6 0.9 copy-start.3
  1.5 23.3 %copy-start = (bf16[1024,16,2,128]{3,2,1,0:T(2,128)(2,1)S(1)}, bf16[1024,16,2,128]{3,2,1,0:T(2,128)(2,1)}, u32[]{:S(2)}) copy-start(bf16[1024,16,2,128]{3,2,1,0:T(2,128)(2,1)} %param.7) | copy-start | bytes 25165828
  1.5 23.3 %copy-start.1 = (bf16[1024,16,2,128]{3,2,1,0:T(2,128)(2,1)S(1)}, bf16[1024,16,2,128]{3,2,1,0:T(2,128)(2,1)}, u32[]{:S(2)}) copy-start(bf16[1024,16,2,128]{3,2,1,0:T(2,128)(2,1)} %param.8) | copy-start | bytes 25165828
  24.9 10.2 %copy-start.2 = (bf16[2048,256]{1,0:T(8,128)(2,1)S(1)}, bf16[2048,256]{1,0:T(8,128)(2,1)}, u32[]{:S(2)}) copy-start(bf16[2048,256]{1,0:T(8,128)(2,1)} %w_ref.1) | copy-start | bytes 3145732
